TPU v7x, 256 devices: a whole 4x4x8 slice. The times are simulated.
256 devices in a mesh: section: 4 (over x), slab: 16 (over z, core), img: 4 (over y).
Axes of the slice: x: 4, y: 4, z: 8, core: 2. Of those that a mesh axis runs over, the one named last changes fastest.
Arguments:
- strips: bfloat16 [4, 4, 8, 128, 320], P('img', None, None, 'slab'), may hold values from -6 to 6
- kernels: bfloat16 [4, 2, 9, 320, 320], P('section'), may hold values from -0.109375 to 0.109375
- cotangent: bfloat16 [4, 4, 8, 128, 320], P('img', None, None, 'slab'), may hold values from -18 to 18
Outputs:
- grad_kernels: float32 [4, 2, 9, 320, 320], P('section', None, None, 'slab', 'img')
- grad_inputs: bfloat16 [4, 4, 4, 8, 128, 320], P('section', 'img', None, None, 'slab')
All inputs are finite; a program needn't handle non-finite values.
Results may differ from a plain program's by a relative error of at most 0.023.
Values may be sent and summed in bfloat16 or wider, within the bound.
A program may use at most 128 MiB of HBM per device.

v0:
```python
import math

import jax
import jax.numpy as jnp
from jax import lax
from jax.experimental import pallas as pl
from jax.experimental.pallas import tpu as pltpu
from jax.sharding import PartitionSpec as P

MESH = pl.DeviceIdType.MESH
F32 = jnp.float32
BF16 = jnp.bfloat16

C = 320
SECTIONS = 4
IMAGES = 4
CROPS = 4
CHIPS = 8
SLABS = 16
ROWS = 8
COLS = 8
POS = ROWS * COLS
WIDE = POS + 16
DEEP = POS + 32
OUT_SHARE = C // IMAGES
IN_SHARE = C // SLABS
HALF = 256
PEERS = 8


def iota(shape, dim):
    return lax.broadcasted_iota(jnp.int32, shape, dim)


def onehot(cond):
    return jnp.where(cond, 1.0, 0.0).astype(BF16)


def sigmoid(v):
    return 1.0 / (1.0 + jnp.exp(-v))


def row_shifts(x):
    count = x.shape[0]
    row = iota(x.shape, 0) % ROWS
    above = jnp.where(row == 0, 0.0, pltpu.roll(x, 1, 0))
    below = jnp.where(row == ROWS - 1, 0.0, pltpu.roll(x, count - 1, 0))
    return above, x, below


def conv(x, weights, part, count):
    shifted = row_shifts(x)
    total = None
    for a in range(3):
        for b in range(3):
            lhs = shifted[a][8 * b : 8 * b + count].astype(BF16)
            term = jnp.dot(lhs, weights[part, 3 * a + b], preferred_element_type=F32)
            total = term if total is None else total + term
    return total


def conv_t(x, weights, part, count):
    shifted = row_shifts(x)
    total = None
    for a in range(3):
        for b in range(3):
            lhs = shifted[a][8 * b : 8 * b + count].astype(BF16)
            term = lax.dot_general(
                lhs,
                weights[part, 8 - (3 * a + b)],
                (((1,), (1,)), ((), ())),
                preferred_element_type=F32,
            )
            total = term if total is None else total + term
    return total


def kernel(
    scaling,
    strips,
    kernels,
    cotangent,
    gk_out,
    gi_out,
    w,
    sv,
    cv,
    fin,
    gin,
    fout,
    gout,
    hid,
    fs,
    fg,
    gs,
    gg,
    cc,
    acc,
    pkl,
    pk,
    rz,
    pc,
    sel,
    c6,
    local_sem,
    fr,
    fsend,
    br,
    bsend,
    edge_send,
    fg_recv,
    fg_send,
    gg_recv,
    gg_send,
    z_recv,
    z_send,
):
    s = lax.axis_index("section")
    slab = lax.axis_index("slab")
    img = lax.axis_index("img")
    z = slab // 2
    core = slab % 2
    has_left = slab > 0
    has_right = slab < SLABS - 1

    loads = [
        pltpu.make_async_copy(strips, sv, local_sem.at[0]),
        pltpu.make_async_copy(cotangent, cv, local_sem.at[1]),
        pltpu.make_async_copy(kernels, w, local_sem.at[2]),
    ]
    for load in loads:
        load.start()

    @pl.when(slab == 0)
    def _():
        for buf in (fin, gin):
            buf[:, 0:16, :] = jnp.zeros((CROPS, 16, C), BF16)

    @pl.when(slab == SLABS - 1)
    def _():
        for buf in (fin, gin):
            buf[:, DEEP - 16 : DEEP, :] = jnp.zeros((CROPS, 16, C), BF16)

    barrier = pltpu.get_barrier_semaphore()

    def greet(where):
        pl.semaphore_signal(barrier, inc=1, device_id=where, device_id_type=MESH)

    def peer_of(m):
        return (s, 2 * z + (core + m % 2) % 2, (img + m // 2) % IMAGES)

    def chip_of(d):
        return (s, 2 * ((z + d) % CHIPS) + core, img)

    greeted = jnp.int32(0)
    for ds in (-1, 0, 1):
        for dj in (-1, 0, 1):
            if ds == 0 and dj == 0:
                continue
            ok = (s + ds >= 0) & (s + ds < SECTIONS) & (slab + dj >= 0) & (slab + dj < SLABS)

            @pl.when(ok)
            def _():
                greet((s + ds, slab + dj, img))

            greeted = greeted + jnp.where(ok, 1, 0)
    for m in range(1, PEERS):
        greet(peer_of(m))
    for d in range(1, CHIPS):
        greet(chip_of(d))
    pl.semaphore_wait(barrier, greeted + (PEERS - 1) + (CHIPS - 1))

    i, j = iota((POS, POS), 0), iota((POS, POS), 1)
    swap = onehot((i // 8 == j % 8) & (i % 8 == j // 8))
    i, j = iota((C, 2 * HALF), 0), iota((C, 2 * HALF), 1)
    lane = j % 32
    pc[...] = onehot((lane < IN_SHARE) & (i == IN_SHARE * (2 * ((j % HALF) // 32) + j // HALF) + lane))
    lane = j % 128
    sel[...] = onehot((lane < OUT_SHARE) & (i == OUT_SHARE * (j // 128) + lane))
    i, j = iota((768, 512), 0), iota((768, 512), 1)
    lane = i % 32
    c6[...] = onehot(
        (lane < IN_SHARE)
        & ((i % 128) // 32 == j // 128)
        & (j % 128 == IN_SHARE * (i // 128) + lane)
    )

    def permuted(x, matrix):
        return jnp.dot(x, matrix, preferred_element_type=F32).astype(BF16)

    def spread(src, dst, send, recv, k, ds, center):
        if center:
            pltpu.make_async_remote_copy(
                src_ref=src.at[k, pl.ds(16, POS)] if src is dst else src.at[k],
                dst_ref=dst.at[k, pl.ds(16, POS)],
                send_sem=send.at[k, 1],
                recv_sem=recv.at[k, 1],
                device_id=(s + ds, slab, img),
                device_id_type=MESH,
            ).start()
        base = 16 if src is dst else 0

        @pl.when(has_right)
        def _():
            pltpu.make_async_remote_copy(
                src_ref=src.at[k, pl.ds(base + POS - 16, 16)],
                dst_ref=dst.at[k, pl.ds(0, 16)],
                send_sem=send.at[k, 2],
                recv_sem=recv.at[k, 0],
                device_id=(s + ds, slab + 1, img),
                device_id_type=MESH,
            ).start()

        @pl.when(has_left)
        def _():
            pltpu.make_async_remote_copy(
                src_ref=src.at[k, pl.ds(base, 16)],
                dst_ref=dst.at[k, pl.ds(DEEP - 16, 16)],
                send_sem=send.at[k, 0],
                recv_sem=recv.at[k, 2],
                device_id=(s + ds, slab - 1, img),
                device_id_type=MESH,
            ).start()

    def waited(ref, sem):
        pltpu.make_async_copy(ref, ref, sem).wait()

    def arrive(dst, recv, k, center):
        @pl.when(center)
        def _():
            waited(dst.at[k, pl.ds(16, POS)], recv.at[k, 1])

        @pl.when(has_left)
        def _():
            waited(dst.at[k, pl.ds(0, 16)], recv.at[k, 0])

        @pl.when(has_right)
        def _():
            waited(dst.at[k, pl.ds(DEEP - 16, 16)], recv.at[k, 2])

    def sent(src, send, k, center):
        base = 16 if center is None else 0
        if center is not None:
            waited(src.at[k], send.at[k, 1])

        @pl.when(has_right)
        def _():
            waited(src.at[k, pl.ds(base + POS - 16, 16)], send.at[k, 2])

        @pl.when(has_left)
        def _():
            waited(src.at[k, pl.ds(base, 16)], send.at[k, 0])

    loads[0].wait()
    loads[1].wait()

    @pl.when(s == 0)
    def _():
        def step(k, carry):
            fin[k, 16 : 16 + POS, :] = permuted(swap, sv[k])
            spread(fin, fin, edge_send, fr, k, 0, False)
            return carry

        lax.fori_loop(0, CROPS, step, 0)

    @pl.when(s == SECTIONS - 1)
    def _():
        def step(k, carry):
            gin[k, 16 : 16 + POS, :] = permuted(swap, cv[k])
            spread(gin, gin, edge_send, br, k, 0, False)
            return carry

        lax.fori_loop(0, CROPS, step, 0)

    loads[2].wait()

    row = iota((WIDE, C), 0)
    inside = jnp.logical_not(
        ((row < 8) & (slab == 0)) | ((row >= WIDE - 8) & (slab == SLABS - 1))
    )

    def share_field(a, k, wide):
        both = permuted(wide, pc[...])
        fs[a, k, 0] = both[:, :HALF]
        fs[a, k, 1] = both[:, HALF:]
        fg[a, k, PEERS - 1] = fs[a, k, core]
        for m in range(1, PEERS):
            pltpu.make_async_remote_copy(
                src_ref=fs.at[a, k, (core + m % 2) % 2],
                dst_ref=fg.at[a, k, m - 1],
                send_sem=fg_send.at[a, k],
                recv_sem=fg_recv.at[a, k],
                device_id=peer_of(m),
                device_id_type=MESH,
            ).start()

    def share_grad(a, k, grad):
        chunks = permuted(grad, sel[...])
        for n in range(IMAGES):
            gs[a, k, n] = chunks[:, 128 * n : 128 * (n + 1)]
        gg[a, k, PEERS - 1] = gs[a, k, img]
        for m in range(1, PEERS):
            pltpu.make_async_remote_copy(
                src_ref=gs.at[a, k, (img + m // 2) % IMAGES],
                dst_ref=gg.at[a, k, m - 1],
                send_sem=gg_send.at[a, k],
                recv_sem=gg_recv.at[a, k],
                device_id=peer_of(m),
                device_id_type=MESH,
            ).start()

    def forward(k, carry):
        arrive(fin, fr, k, s > 0)
        x = fin[k].astype(F32)
        hidden = conv(x, w, 0, WIDE)
        hid[k] = hidden
        active = jnp.where(inside, hidden * sigmoid(hidden), 0.0).astype(BF16)

        @pl.when(s < SECTIONS - 1)
        def _():
            result = x[16 : 16 + POS] + conv(active.astype(F32), w, 1, POS)
            fout[k] = result.astype(BF16)
            spread(fout, fin, fsend, fr, k, 1, True)

        share_field(0, k, x[8 : 8 + WIDE].astype(BF16))
        share_field(1, k, active)
        return carry

    lax.fori_loop(0, CROPS, forward, 0)

    def backward(k, carry):
        arrive(gin, br, k, s < SECTIONS - 1)
        g = gin[k].astype(F32)
        grad_active = conv_t(g, w, 1, WIDE)
        hidden = hid[k]
        q = sigmoid(hidden)
        slope = q * (1.0 + hidden * (1.0 - q))
        grad_hidden = jnp.where(inside, grad_active * slope, 0.0).astype(BF16)
        wide = grad_hidden.astype(F32)
        center = g[16 : 16 + POS]
        grad_in = (center + conv_t(wide, w, 0, POS)).astype(BF16)
        gout[k] = grad_in

        @pl.when(s > 0)
        def _():
            spread(gout, gin, bsend, br, k, -1, True)

        gi_out[k] = permuted(swap, grad_in)
        share_grad(1, k, center.astype(BF16))
        share_grad(0, k, wide[8 : 8 + POS].astype(BF16))
        return carry

    lax.fori_loop(0, CROPS, backward, 0)

    acc[...] = jnp.zeros_like(acc)

    def contract(n, carry):
        a, k = n // CROPS, n % CROPS
        waited(fg.at[a, k, pl.ds(0, PEERS - 1)], fg_recv.at[a, k])
        waited(gg.at[a, k, pl.ds(0, PEERS - 1)], gg_recv.at[a, k])

        def unfold(m, carry):
            shifted = row_shifts(fg[a, k, m].astype(F32))
            for d in range(3):
                for b in range(3):
                    cc[3 * d + b, pl.ds(pl.multiple_of(m * POS, POS), POS), :] = shifted[d][
                        8 * b : 8 * b + POS
                    ].astype(BF16)
            return carry

        lax.fori_loop(0, PEERS, unfold, 0)
        grads = gg[a, k].reshape(PEERS * POS, 128).T

        def tap(t, carry):
            acc[a, t] += jnp.dot(grads, cc[t], preferred_element_type=F32)
            return carry

        lax.fori_loop(0, 9, tap, 0)
        return carry

    lax.fori_loop(0, 2 * CROPS, contract, 0)

    for t in range(3):
        for p in range(6):
            a, tap = divmod(6 * t + p, 9)
            block = acc[a, tap, 0:OUT_SHARE, :].astype(BF16)
            for half in range(2):
                pkl[2 * t + half, :, 128 * p : 128 * (p + 1)] = block[:, 128 * half : 128 * (half + 1)]
    for n in range(6):
        t, half = divmod(n, 2)
        packed = permuted(pkl[n], c6[...])
        for q in range(4):
            pk[4 * half + q, t] = packed[:, 128 * q : 128 * (q + 1)]
    for d in range(1, CHIPS):
        pltpu.make_async_remote_copy(
            src_ref=pk.at[(z + d) % CHIPS],
            dst_ref=rz.at[d - 1],
            send_sem=z_send,
            recv_sem=z_recv,
            device_id=chip_of(d),
            device_id_type=MESH,
        ).start()
    waited(rz, z_recv)
    for t in range(3):
        total = pk[z, t].astype(F32)
        for d in range(CHIPS - 1):
            total = total + rz[d, t].astype(F32)
        gk_out[t] = (total * scaling).T

    waited(rz, z_send)

    def drain(k, carry):
        @pl.when(s == 0)
        def _():
            sent(fin, edge_send, k, None)

        @pl.when(s == SECTIONS - 1)
        def _():
            sent(gin, edge_send, k, None)

        @pl.when(s < SECTIONS - 1)
        def _():
            sent(fout, fsend, k, True)

        @pl.when(s > 0)
        def _():
            sent(gout, bsend, k, True)

        for a in range(2):
            waited(fg.at[a, k, pl.ds(0, PEERS - 1)], fg_send.at[a, k])
            waited(gg.at[a, k, pl.ds(0, PEERS - 1)], gg_send.at[a, k])
        return carry

    lax.fori_loop(0, CROPS, drain, 0)


def shards(strips, kernels, cotangent):
    scaling = 1.0 / math.sqrt(IMAGES * CROPS * ROWS * COLS * SLABS)
    dma = pltpu.SemaphoreType.DMA
    vmem = pl.BlockSpec(memory_space=pltpu.VMEM)
    hbm = pl.BlockSpec(memory_space=pl.ANY)
    gk, gi = pl.pallas_call(
        lambda *refs: kernel(scaling, *refs),
        out_shape=(
            jax.ShapeDtypeStruct((3, 128, OUT_SHARE), F32),
            jax.ShapeDtypeStruct((CROPS, POS, C), BF16),
        ),
        in_specs=[hbm, hbm, hbm],
        out_specs=(vmem, vmem),
        scratch_shapes=[
            pltpu.VMEM((2, 9, C, C), BF16),
            pltpu.VMEM((CROPS, POS, C), BF16),
            pltpu.VMEM((CROPS, POS, C), BF16),
            pltpu.VMEM((CROPS, DEEP, C), BF16),
            pltpu.VMEM((CROPS, DEEP, C), BF16),
            pltpu.VMEM((CROPS, POS, C), BF16),
            pltpu.VMEM((CROPS, POS, C), BF16),
            pltpu.VMEM((CROPS, WIDE, C), F32),
            pltpu.VMEM((2, CROPS, 2, WIDE, HALF), BF16),
            pltpu.VMEM((2, CROPS, PEERS, WIDE, HALF), BF16),
            pltpu.VMEM((2, CROPS, IMAGES, POS, 128), BF16),
            pltpu.VMEM((2, CROPS, PEERS, POS, 128), BF16),
            pltpu.VMEM((9, PEERS * POS, HALF), BF16),
            pltpu.VMEM((2, 9, 128, HALF), F32),
            pltpu.VMEM((6, OUT_SHARE, 768), BF16),
            pltpu.VMEM((CHIPS, 3, OUT_SHARE, 128), BF16),
            pltpu.VMEM((CHIPS - 1, 3, OUT_SHARE, 128), BF16),
            pltpu.VMEM((C, 2 * HALF), BF16),
            pltpu.VMEM((C, 512), BF16),
            pltpu.VMEM((768, 512), BF16),
            dma((3,)),
            dma((CROPS, 3)),
            dma((CROPS, 3)),
            dma((CROPS, 3)),
            dma((CROPS, 3)),
            dma((CROPS, 3)),
            dma((2, CROPS)),
            dma((2, CROPS)),
            dma((2, CROPS)),
            dma((2, CROPS)),
            dma,
            dma,
        ],
        compiler_params=pltpu.CompilerParams(
            collective_id=0, has_side_effects=True, vmem_limit_bytes=60 * 1024 * 1024
        ),
        name="residual_step",
    )(
        strips.reshape(CROPS, POS, C),
        kernels.reshape(2, 9, C, C),
        cotangent.reshape(CROPS, POS, C),
    )
    grad_kernels = gk[:, : 6 * IN_SHARE].reshape(1, 2, 9, IN_SHARE, OUT_SHARE)
    return grad_kernels, gi.reshape(1, 1, CROPS, ROWS, COLS, C)


def solution(mesh):
    return jax.shard_map(
        shards,
        mesh=mesh,
        in_specs=(
            P("img", None, None, "slab", None),
            P("section", None, None, None, None),
            P("img", None, None, "slab", None),
        ),
        out_specs=(
            P("section", None, None, "slab", "img"),
            P("section", "img", None, None, "slab", None),
        ),
        check_vma=False,
    )
```

profile of v0, /device:TPU:1, one launch (start us, length us, event | category | flops | bytes accessed | tf_op | source)
XLA Modules:
  0.0 97.8 jit_solution(5920028534911470441)
XLA Ops:
  0.6 93.8 %residual_step.1 = (f32[3,128,80]{2,1,0:T(8,128)}, bf16[4,64,320]{2,1,0:T(8,128)(2,1)}) custom-call(bf16[4,64,320]{2,1,0:T(8,128)(2,1)} %bitcast.5, bf16[2,9,320,320]{3,2,1,0:T(8,128)(2,1)} %bitcast.4, bf16[4,64,320]{2,1,0:T(8,128)(2,1)} %bitcast.6), custom_call_target="tpu_custom_call" | custom-call | tf_op jit(solution)/shard_map/residual_step/pallas_call | solution.py:442
  94.4 0.9 slice.3
  95.4 0.8 copy.6
  96.2 1.6 %copy.8 = bf16[1,1,4,8,8,320]{5,4,3,2,1,0:T(8,128)(2,1)} copy(bf16[1,1,4,8,8,320]{5,4,3,2,1,0:T(8,128)(2,1)} %bitcast.7) | data formatting | bytes 327680
  (1 shorter events, 0.0 us)
where the time goes:
time: 99.1 us; the launch traced here: 97.8 us
  Pallas kernels  93.8 us (95%)
  local copies, waits for them, and re-layouts  3.35 us (3%)
    pallas_call x1, Pallas kernels, shards(): pl.pallas_call(lambda *refs: kernel(scaling, *refs), out_shape=(jax.Shape...  93.8 us
    unnamed x2, local copies, waits for them, and re-layouts  2.39 us

commit v1 on v0

--- a/solution.py
+++ b/solution.py
@@ -59,22 +59,6 @@
     return total
 
 
-def conv_t(x, weights, part, count):
-    shifted = row_shifts(x)
-    total = None
-    for a in range(3):
-        for b in range(3):
-            lhs = shifted[a][8 * b : 8 * b + count].astype(BF16)
-            term = lax.dot_general(
-                lhs,
-                weights[part, 8 - (3 * a + b)],
-                (((1,), (1,)), ((), ())),
-                preferred_element_type=F32,
-            )
-            total = term if total is None else total + term
-    return total
-
-
 def kernel(
     scaling,
     strips,
@@ -83,8 +67,10 @@
     gk_out,
     gi_out,
     w,
+    wt,
     sv,
     cv,
+    gi,
     fin,
     gin,
     fout,
@@ -103,6 +89,8 @@
     sel,
     c6,
     local_sem,
+    weight_sem,
+    gi_sem,
     fr,
     fsend,
     br,
@@ -126,8 +114,14 @@
     loads = [
         pltpu.make_async_copy(strips, sv, local_sem.at[0]),
         pltpu.make_async_copy(cotangent, cv, local_sem.at[1]),
-        pltpu.make_async_copy(kernels, w, local_sem.at[2]),
     ]
+    for part in range(2):
+        for tap in range(9):
+            loads.append(
+                pltpu.make_async_copy(
+                    kernels.at[part, tap], w.at[part, tap], weight_sem.at[part, tap]
+                )
+            )
     for load in loads:
         load.start()
 
@@ -168,8 +162,6 @@
         greet(peer_of(m))
     for d in range(1, CHIPS):
         greet(chip_of(d))
-    pl.semaphore_wait(barrier, greeted + (PEERS - 1) + (CHIPS - 1))
-
     i, j = iota((POS, POS), 0), iota((POS, POS), 1)
     swap = onehot((i // 8 == j % 8) & (i % 8 == j // 8))
     i, j = iota((C, 2 * HALF), 0), iota((C, 2 * HALF), 1)
@@ -185,19 +177,13 @@
         & (j % 128 == IN_SHARE * (i // 128) + lane)
     )
 
+    acc[...] = jnp.zeros_like(acc)
+    pl.semaphore_wait(barrier, greeted + (PEERS - 1) + (CHIPS - 1))
+
     def permuted(x, matrix):
         return jnp.dot(x, matrix, preferred_element_type=F32).astype(BF16)
 
     def spread(src, dst, send, recv, k, ds, center):
-        if center:
-            pltpu.make_async_remote_copy(
-                src_ref=src.at[k, pl.ds(16, POS)] if src is dst else src.at[k],
-                dst_ref=dst.at[k, pl.ds(16, POS)],
-                send_sem=send.at[k, 1],
-                recv_sem=recv.at[k, 1],
-                device_id=(s + ds, slab, img),
-                device_id_type=MESH,
-            ).start()
         base = 16 if src is dst else 0
 
         @pl.when(has_right)
@@ -222,6 +208,16 @@
                 device_id_type=MESH,
             ).start()
 
+        if center:
+            pltpu.make_async_remote_copy(
+                src_ref=src.at[k],
+                dst_ref=dst.at[k, pl.ds(16, POS)],
+                send_sem=send.at[k, 1],
+                recv_sem=recv.at[k, 1],
+                device_id=(s + ds, slab, img),
+                device_id_type=MESH,
+            ).start()
+
     def waited(ref, sem):
         pltpu.make_async_copy(ref, ref, sem).wait()
 
@@ -272,7 +268,18 @@
 
         lax.fori_loop(0, CROPS, step, 0)
 
-    loads[2].wait()
+    for load in loads[2:]:
+        load.wait()
+
+    def transpose_weights():
+        def step(n, carry):
+            part, tap = n // 9, n % 9
+            wt[part, 8 - tap] = w[part, tap].T
+            return carry
+
+        lax.fori_loop(0, 18, step, 0)
+
+    pl.when(s > 0)(transpose_weights)
 
     row = iota((WIDE, C), 0)
     inside = jnp.logical_not(
@@ -327,58 +334,83 @@
         return carry
 
     lax.fori_loop(0, CROPS, forward, 0)
-
-    def backward(k, carry):
+    pl.when(s == 0)(transpose_weights)
+
+    def backward(k):
         arrive(gin, br, k, s < SECTIONS - 1)
         g = gin[k].astype(F32)
-        grad_active = conv_t(g, w, 1, WIDE)
+        grad_active = conv(g, wt, 1, WIDE)
         hidden = hid[k]
         q = sigmoid(hidden)
         slope = q * (1.0 + hidden * (1.0 - q))
         grad_hidden = jnp.where(inside, grad_active * slope, 0.0).astype(BF16)
         wide = grad_hidden.astype(F32)
         center = g[16 : 16 + POS]
-        grad_in = (center + conv_t(wide, w, 0, POS)).astype(BF16)
+        grad_in = (center + conv(wide, wt, 0, POS)).astype(BF16)
         gout[k] = grad_in
 
         @pl.when(s > 0)
         def _():
             spread(gout, gin, bsend, br, k, -1, True)
 
-        gi_out[k] = permuted(swap, grad_in)
+        gi[k] = permuted(swap, grad_in)
+        pltpu.make_async_copy(gi.at[k], gi_out.at[k], gi_sem.at[k]).start()
         share_grad(1, k, center.astype(BF16))
         share_grad(0, k, wide[8 : 8 + POS].astype(BF16))
+
+    def unfold(k):
+        for a in range(2):
+            waited(fg.at[a, k, pl.ds(0, PEERS - 1)], fg_recv.at[a, k])
+
+            def source(m, carry):
+                shifted = row_shifts(fg[a, k, m].astype(F32))
+                for d in range(3):
+                    for b in range(3):
+                        cc[a, k, 3 * d + b, pl.ds(pl.multiple_of(m * POS, POS), POS), :] = shifted[d][
+                            8 * b : 8 * b + POS
+                        ].astype(BF16)
+                return carry
+
+            lax.fori_loop(0, PEERS, source, 0)
+
+    def contract(k):
+        for a in range(2):
+            waited(gg.at[a, k, pl.ds(0, PEERS - 1)], gg_recv.at[a, k])
+            grads = gg[a, k].reshape(PEERS * POS, 128).T
+
+            def tap(t, carry):
+                acc[a, t] += jnp.dot(grads, cc[a, k, t], preferred_element_type=F32)
+                return carry
+
+            lax.fori_loop(0, 9, tap, 0)
+
+    last = CROPS - 1
+    early = s < 2
+
+    def middle(i, carry):
+        unfolding = jnp.where(early, i < last, i >= CROPS)
+
+        @pl.when(unfolding)
+        def _():
+            unfold(jnp.where(early, i, i - CROPS))
+
+        @pl.when(jnp.logical_not(unfolding))
+        def _():
+            backward(jnp.where(early, i - last, i))
+
         return carry
 
-    lax.fori_loop(0, CROPS, backward, 0)
-
-    acc[...] = jnp.zeros_like(acc)
-
-    def contract(n, carry):
-        a, k = n // CROPS, n % CROPS
-        waited(fg.at[a, k, pl.ds(0, PEERS - 1)], fg_recv.at[a, k])
-        waited(gg.at[a, k, pl.ds(0, PEERS - 1)], gg_recv.at[a, k])
-
-        def unfold(m, carry):
-            shifted = row_shifts(fg[a, k, m].astype(F32))
-            for d in range(3):
-                for b in range(3):
-                    cc[3 * d + b, pl.ds(pl.multiple_of(m * POS, POS), POS), :] = shifted[d][
-                        8 * b : 8 * b + POS
-                    ].astype(BF16)
-            return carry
-
-        lax.fori_loop(0, PEERS, unfold, 0)
-        grads = gg[a, k].reshape(PEERS * POS, 128).T
-
-        def tap(t, carry):
-            acc[a, t] += jnp.dot(grads, cc[t], preferred_element_type=F32)
-            return carry
-
-        lax.fori_loop(0, 9, tap, 0)
+    lax.fori_loop(0, CROPS + last, middle, 0)
+
+    def finish(k, carry):
+        @pl.when(k == last)
+        def _():
+            unfold(k)
+
+        contract(k)
         return carry
 
-    lax.fori_loop(0, 2 * CROPS, contract, 0)
+    lax.fori_loop(0, CROPS, finish, 0)
 
     for t in range(3):
         for p in range(6):
@@ -386,11 +418,14 @@
             block = acc[a, tap, 0:OUT_SHARE, :].astype(BF16)
             for half in range(2):
                 pkl[2 * t + half, :, 128 * p : 128 * (p + 1)] = block[:, 128 * half : 128 * (half + 1)]
-    for n in range(6):
-        t, half = divmod(n, 2)
-        packed = permuted(pkl[n], c6[...])
-        for q in range(4):
-            pk[4 * half + q, t] = packed[:, 128 * q : 128 * (q + 1)]
+    for pair in range(2):
+        packed = permuted(
+            pkl[...].reshape(6 * OUT_SHARE, 768), c6[:, 256 * pair : 256 * (pair + 1)]
+        ).reshape(6, OUT_SHARE, 256)
+        for t in range(3):
+            for half in range(2):
+                for q in range(2):
+                    pk[4 * half + 2 * pair + q, t] = packed[2 * t + half, :, 128 * q : 128 * (q + 1)]
     for d in range(1, CHIPS):
         pltpu.make_async_remote_copy(
             src_ref=pk.at[(z + d) % CHIPS],
@@ -405,11 +440,16 @@
         total = pk[z, t].astype(F32)
         for d in range(CHIPS - 1):
             total = total + rz[d, t].astype(F32)
-        gk_out[t] = (total * scaling).T
+        flipped = (total * scaling).T
+        for p in range(6):
+            a, tap = divmod(6 * t + p, 9)
+            gk_out[a, tap] = flipped[IN_SHARE * p : IN_SHARE * (p + 1)]
 
     waited(rz, z_send)
 
     def drain(k, carry):
+        pltpu.make_async_copy(gi.at[k], gi_out.at[k], gi_sem.at[k]).wait()
+
         @pl.when(s == 0)
         def _():
             sent(fin, edge_send, k, None)
@@ -442,13 +482,15 @@
     gk, gi = pl.pallas_call(
         lambda *refs: kernel(scaling, *refs),
         out_shape=(
-            jax.ShapeDtypeStruct((3, 128, OUT_SHARE), F32),
+            jax.ShapeDtypeStruct((2, 9, IN_SHARE, OUT_SHARE), F32),
             jax.ShapeDtypeStruct((CROPS, POS, C), BF16),
         ),
         in_specs=[hbm, hbm, hbm],
-        out_specs=(vmem, vmem),
+        out_specs=(vmem, hbm),
         scratch_shapes=[
             pltpu.VMEM((2, 9, C, C), BF16),
+            pltpu.VMEM((2, 9, C, C), BF16),
+            pltpu.VMEM((CROPS, POS, C), BF16),
             pltpu.VMEM((CROPS, POS, C), BF16),
             pltpu.VMEM((CROPS, POS, C), BF16),
             pltpu.VMEM((CROPS, DEEP, C), BF16),
@@ -460,7 +502,7 @@
             pltpu.VMEM((2, CROPS, PEERS, WIDE, HALF), BF16),
             pltpu.VMEM((2, CROPS, IMAGES, POS, 128), BF16),
             pltpu.VMEM((2, CROPS, PEERS, POS, 128), BF16),
-            pltpu.VMEM((9, PEERS * POS, HALF), BF16),
+            pltpu.VMEM((2, CROPS, 9, PEERS * POS, HALF), BF16),
             pltpu.VMEM((2, 9, 128, HALF), F32),
             pltpu.VMEM((6, OUT_SHARE, 768), BF16),
             pltpu.VMEM((CHIPS, 3, OUT_SHARE, 128), BF16),
@@ -468,7 +510,9 @@
             pltpu.VMEM((C, 2 * HALF), BF16),
             pltpu.VMEM((C, 512), BF16),
             pltpu.VMEM((768, 512), BF16),
-            dma((3,)),
+            dma((2,)),
+            dma((2, 9)),
+            dma((CROPS,)),
             dma((CROPS, 3)),
             dma((CROPS, 3)),
             dma((CROPS, 3)),
@@ -490,8 +534,7 @@
         kernels.reshape(2, 9, C, C),
         cotangent.reshape(CROPS, POS, C),
     )
-    grad_kernels = gk[:, : 6 * IN_SHARE].reshape(1, 2, 9, IN_SHARE, OUT_SHARE)
-    return grad_kernels, gi.reshape(1, 1, CROPS, ROWS, COLS, C)
+    return gk[None], gi.reshape(1, 1, CROPS, ROWS, COLS, C)
 
 
 def solution(mesh):

time: 99.1 us -> 96.1 us (0.970)
  the two profiles are of different devices: /device:TPU:1 before, /device:TPU:6 now
where the time goes in v1:
time: 96.1 us; the launch traced here: 95.9 us
  Pallas kernels  92 us (96%)
  local copies, waits for them, and re-layouts  3.33 us (3%)
    pallas_call x1, Pallas kernels, shards(): pl.pallas_call(lambda *refs: kernel(scaling, *refs), out_shape=(jax.Shape...  92 us
    unnamed x2, local copies, waits for them, and re-layouts  3.33 us

profile of v1, /device:TPU:6, one launch (start us, length us, event | category | flops | bytes accessed | tf_op | source)
XLA Modules:
  0.0 95.9 jit_solution(18221174914994182723)
XLA Ops:
  0.6 92.0 %residual_step.1 = (f32[2,9,20,80]{3,2,1,0:T(8,128)}, bf16[4,64,320]{2,1,0:T(8,128)(2,1)}) custom-call(bf16[4,64,320]{2,1,0:T(8,128)(2,1)} %bitcast.7, bf16[2,9,320,320]{3,2,1,0:T(8,128)(2,1)} %bitcast.5, bf16[4,64,320]{2,1,0:T(8,128)(2,1)} %bitcast.8), custom_call_target="tpu_custom_call" | custom-call | tf_op jit(solution)/shard_map/residual_step/pallas_call | solution.py:482
  92.6 1.7 %copy.5 = f32[1,2,9,20,80]{4,1,3,2,0:T(2,128)} copy(f32[1,2,9,20,80]{4,3,2,1,0:T(8,128)} %bitcast.6) | data formatting | bytes 230400
  94.3 1.6 %copy.7 = bf16[1,1,4,8,8,320]{5,4,3,2,1,0:T(8,128)(2,1)} copy(bf16[1,1,4,8,8,320]{5,4,3,2,1,0:T(8,128)(2,1)} %bitcast.9) | data formatting | bytes 327680

commit v2 on v1

--- a/solution.py
+++ b/solution.py
@@ -76,6 +76,7 @@
     fout,
     gout,
     hid,
+    raw,
     fs,
     fg,
     gs,
@@ -96,10 +97,14 @@
     br,
     bsend,
     edge_send,
+    raw_recv,
+    raw_send,
     fg_recv,
     fg_send,
     gg_recv,
     gg_send,
+    gr_recv,
+    gr_send,
     z_recv,
     z_send,
 ):
@@ -140,8 +145,10 @@
     def greet(where):
         pl.semaphore_signal(barrier, inc=1, device_id=where, device_id_type=MESH)
 
-    def peer_of(m):
-        return (s, 2 * z + (core + m % 2) % 2, (img + m // 2) % IMAGES)
+    def image_of(d):
+        return (s, slab, (img + d) % IMAGES)
+
+    partner = (s, 2 * z + 1 - core, img)
 
     def chip_of(d):
         return (s, 2 * ((z + d) % CHIPS) + core, img)
@@ -158,17 +165,20 @@
                 greet((s + ds, slab + dj, img))
 
             greeted = greeted + jnp.where(ok, 1, 0)
-    for m in range(1, PEERS):
-        greet(peer_of(m))
+    for d in range(1, IMAGES):
+        greet(image_of(d))
+    greet(partner)
     for d in range(1, CHIPS):
         greet(chip_of(d))
     i, j = iota((POS, POS), 0), iota((POS, POS), 1)
     swap = onehot((i // 8 == j % 8) & (i % 8 == j // 8))
     i, j = iota((C, 2 * HALF), 0), iota((C, 2 * HALF), 1)
     lane = j % 32
-    pc[...] = onehot((lane < IN_SHARE) & (i == IN_SHARE * (2 * ((j % HALF) // 32) + j // HALF) + lane))
+    side = (j // HALF + core) % 2
+    pc[...] = onehot((lane < IN_SHARE) & (i == IN_SHARE * (2 * ((j % HALF) // 32) + side) + lane))
     lane = j % 128
-    sel[...] = onehot((lane < OUT_SHARE) & (i == OUT_SHARE * (j // 128) + lane))
+    owner = (j // 128 + img) % IMAGES
+    sel[...] = onehot((lane < OUT_SHARE) & (i == OUT_SHARE * owner + lane))
     i, j = iota((768, 512), 0), iota((768, 512), 1)
     lane = i % 32
     c6[...] = onehot(
@@ -178,7 +188,7 @@
     )
 
     acc[...] = jnp.zeros_like(acc)
-    pl.semaphore_wait(barrier, greeted + (PEERS - 1) + (CHIPS - 1))
+    pl.semaphore_wait(barrier, greeted + IMAGES + (CHIPS - 1))
 
     def permuted(x, matrix):
         return jnp.dot(x, matrix, preferred_element_type=F32).astype(BF16)
@@ -287,34 +297,57 @@
     )
 
     def share_field(a, k, wide):
-        both = permuted(wide, pc[...])
-        fs[a, k, 0] = both[:, :HALF]
-        fs[a, k, 1] = both[:, HALF:]
-        fg[a, k, PEERS - 1] = fs[a, k, core]
-        for m in range(1, PEERS):
+        raw[a, k, IMAGES - 1] = wide
+        for d in range(1, IMAGES):
             pltpu.make_async_remote_copy(
-                src_ref=fs.at[a, k, (core + m % 2) % 2],
-                dst_ref=fg.at[a, k, m - 1],
+                src_ref=raw.at[a, k, IMAGES - 1],
+                dst_ref=raw.at[a, k, d - 1],
+                send_sem=raw_send.at[a, k],
+                recv_sem=raw_recv.at[a, k],
+                device_id=image_of(d),
+                device_id_type=MESH,
+            ).start()
+
+    def relay_field(k):
+        for a in range(2):
+            waited(raw.at[a, k, pl.ds(0, IMAGES - 1)], raw_recv.at[a, k])
+            for n in range(IMAGES):
+                both = permuted(raw[a, k, n], pc[...])
+                fg[a, k, n] = both[:, :HALF]
+                fs[a, k, n] = both[:, HALF:]
+            pltpu.make_async_remote_copy(
+                src_ref=fs.at[a, k],
+                dst_ref=fg.at[a, k, pl.ds(IMAGES, IMAGES)],
                 send_sem=fg_send.at[a, k],
                 recv_sem=fg_recv.at[a, k],
-                device_id=peer_of(m),
+                device_id=partner,
                 device_id_type=MESH,
             ).start()
 
     def share_grad(a, k, grad):
         chunks = permuted(grad, sel[...])
-        for n in range(IMAGES):
-            gs[a, k, n] = chunks[:, 128 * n : 128 * (n + 1)]
-        gg[a, k, PEERS - 1] = gs[a, k, img]
-        for m in range(1, PEERS):
+        gg[a, k, IMAGES - 1] = chunks[:, :128]
+        for d in range(1, IMAGES):
+            gs[a, k, d - 1] = chunks[:, 128 * d : 128 * (d + 1)]
             pltpu.make_async_remote_copy(
-                src_ref=gs.at[a, k, (img + m // 2) % IMAGES],
-                dst_ref=gg.at[a, k, m - 1],
+                src_ref=gs.at[a, k, d - 1],
+                dst_ref=gg.at[a, k, d - 1],
                 send_sem=gg_send.at[a, k],
                 recv_sem=gg_recv.at[a, k],
-                device_id=peer_of(m),
+                device_id=image_of(d),
                 device_id_type=MESH,
             ).start()
+
+    def relay_grad(a, k):
+        waited(gg.at[a, k, pl.ds(0, IMAGES - 1)], gg_recv.at[a, k])
+        pltpu.make_async_remote_copy(
+            src_ref=gg.at[a, k, pl.ds(0, IMAGES)],
+            dst_ref=gg.at[a, k, pl.ds(IMAGES, IMAGES)],
+            send_sem=gr_send.at[a, k],
+            recv_sem=gr_recv.at[a, k],
+            device_id=partner,
+            device_id_type=MESH,
+        ).start()
 
     def forward(k, carry):
         arrive(fin, fr, k, s > 0)
@@ -360,7 +393,7 @@
 
     def unfold(k):
         for a in range(2):
-            waited(fg.at[a, k, pl.ds(0, PEERS - 1)], fg_recv.at[a, k])
+            waited(fg.at[a, k, pl.ds(IMAGES, IMAGES)], fg_recv.at[a, k])
 
             def source(m, carry):
                 shifted = row_shifts(fg[a, k, m].astype(F32))
@@ -373,79 +406,102 @@
 
             lax.fori_loop(0, PEERS, source, 0)
 
-    def contract(k):
-        for a in range(2):
-            waited(gg.at[a, k, pl.ds(0, PEERS - 1)], gg_recv.at[a, k])
-            grads = gg[a, k].reshape(PEERS * POS, 128).T
-
-            def tap(t, carry):
-                acc[a, t] += jnp.dot(grads, cc[a, k, t], preferred_element_type=F32)
-                return carry
-
-            lax.fori_loop(0, 9, tap, 0)
-
-    last = CROPS - 1
+    def contract(a, k):
+        waited(gg.at[a, k, pl.ds(IMAGES, IMAGES)], gr_recv.at[a, k])
+        grads = gg[a, k].reshape(PEERS * POS, 128).T[:OUT_SHARE]
+        for t in range(9):
+            acc[a, t] += jnp.dot(grads, cc[a, k, t], preferred_element_type=F32)
+
     early = s < 2
 
+    def unfold_step(n):
+        @pl.when(n < CROPS)
+        def _():
+            relay_field(n)
+
+        @pl.when(n > 0)
+        def _():
+            unfold(n - 1)
+
     def middle(i, carry):
-        unfolding = jnp.where(early, i < last, i >= CROPS)
+        unfolding = jnp.where(early, i <= CROPS, i >= CROPS)
 
         @pl.when(unfolding)
         def _():
-            unfold(jnp.where(early, i, i - CROPS))
+            unfold_step(jnp.where(early, i, i - CROPS))
 
         @pl.when(jnp.logical_not(unfolding))
         def _():
-            backward(jnp.where(early, i - last, i))
+            backward(jnp.where(early, i - CROPS - 1, i))
 
         return carry
 
-    lax.fori_loop(0, CROPS + last, middle, 0)
-
-    def finish(k, carry):
-        @pl.when(k == last)
-        def _():
-            unfold(k)
-
-        contract(k)
-        return carry
-
-    lax.fori_loop(0, CROPS, finish, 0)
-
-    for t in range(3):
+    lax.fori_loop(0, 2 * CROPS + 1, middle, 0)
+
+    def pack(t):
         for p in range(6):
             a, tap = divmod(6 * t + p, 9)
-            block = acc[a, tap, 0:OUT_SHARE, :].astype(BF16)
+            block = acc[a, tap].astype(BF16)
             for half in range(2):
-                pkl[2 * t + half, :, 128 * p : 128 * (p + 1)] = block[:, 128 * half : 128 * (half + 1)]
-    for pair in range(2):
-        packed = permuted(
-            pkl[...].reshape(6 * OUT_SHARE, 768), c6[:, 256 * pair : 256 * (pair + 1)]
-        ).reshape(6, OUT_SHARE, 256)
-        for t in range(3):
-            for half in range(2):
-                for q in range(2):
-                    pk[4 * half + 2 * pair + q, t] = packed[2 * t + half, :, 128 * q : 128 * (q + 1)]
-    for d in range(1, CHIPS):
-        pltpu.make_async_remote_copy(
-            src_ref=pk.at[(z + d) % CHIPS],
-            dst_ref=rz.at[d - 1],
-            send_sem=z_send,
-            recv_sem=z_recv,
-            device_id=chip_of(d),
-            device_id_type=MESH,
-        ).start()
-    waited(rz, z_recv)
-    for t in range(3):
-        total = pk[z, t].astype(F32)
+                pkl[t, half, :, 128 * p : 128 * (p + 1)] = block[:, 128 * half : 128 * (half + 1)]
+        packed = permuted(pkl[t].reshape(2 * OUT_SHARE, 768), c6[...]).reshape(2, OUT_SHARE, 512)
+        for half in range(2):
+            for q in range(4):
+                pk[t, 4 * half + q] = packed[half, :, 128 * q : 128 * (q + 1)]
+        for d in range(1, CHIPS):
+            pltpu.make_async_remote_copy(
+                src_ref=pk.at[t, (z + d) % CHIPS],
+                dst_ref=rz.at[t, d - 1],
+                send_sem=z_send.at[t],
+                recv_sem=z_recv.at[t],
+                device_id=chip_of(d),
+                device_id_type=MESH,
+            ).start()
+
+    last = CROPS - 1
+
+    def hand_over(k, carry):
+        relay_grad(1, k)
+        relay_grad(0, k)
+        return carry
+
+    lax.fori_loop(0, last, hand_over, 0)
+
+    def tail(i, carry):
+        @pl.when(i == 3)
+        def _():
+            relay_grad(1, last)
+
+        @pl.when(i == 4)
+        def _():
+            relay_grad(0, last)
+
+        upper = (i < 3) | (i == 5)
+        crop = jnp.where(i < 3, i, jnp.where(i < 5, i - 3, jnp.where(i == 5, last, i - 4)))
+        contract(jnp.where(upper, 1, 0), crop)
+
+        @pl.when(i == 5)
+        def _():
+            pack(2)
+
+        return carry
+
+    lax.fori_loop(0, 2 * CROPS, tail, 0)
+    pack(1)
+    pack(0)
+
+    for t in (2, 1, 0):
+        waited(rz.at[t], z_recv.at[t])
+        total = pk[t, z].astype(F32)
         for d in range(CHIPS - 1):
-            total = total + rz[d, t].astype(F32)
+            total = total + rz[t, d].astype(F32)
         flipped = (total * scaling).T
         for p in range(6):
             a, tap = divmod(6 * t + p, 9)
             gk_out[a, tap] = flipped[IN_SHARE * p : IN_SHARE * (p + 1)]
 
-    waited(rz, z_send)
+    for t in range(3):
+        waited(rz.at[t], z_send.at[t])
 
     def drain(k, carry):
         pltpu.make_async_copy(gi.at[k], gi_out.at[k], gi_sem.at[k]).wait()
@@ -467,8 +523,10 @@
             sent(gout, bsend, k, True)
 
         for a in range(2):
-            waited(fg.at[a, k, pl.ds(0, PEERS - 1)], fg_send.at[a, k])
-            waited(gg.at[a, k, pl.ds(0, PEERS - 1)], gg_send.at[a, k])
+            waited(raw.at[a, k, pl.ds(0, IMAGES - 1)], raw_send.at[a, k])
+            waited(fs.at[a, k], fg_send.at[a, k])
+            waited(gs.at[a, k], gg_send.at[a, k])
+            waited(gg.at[a, k, pl.ds(0, IMAGES)], gr_send.at[a, k])
         return carry
 
     lax.fori_loop(0, CROPS, drain, 0)
@@ -498,15 +556,16 @@
             pltpu.VMEM((CROPS, POS, C), BF16),
             pltpu.VMEM((CROPS, POS, C), BF16),
             pltpu.VMEM((CROPS, WIDE, C), F32),
-            pltpu.VMEM((2, CROPS, 2, WIDE, HALF), BF16),
+            pltpu.VMEM((2, CROPS, IMAGES, WIDE, C), BF16),
+            pltpu.VMEM((2, CROPS, IMAGES, WIDE, HALF), BF16),
             pltpu.VMEM((2, CROPS, PEERS, WIDE, HALF), BF16),
-            pltpu.VMEM((2, CROPS, IMAGES, POS, 128), BF16),
+            pltpu.VMEM((2, CROPS, IMAGES - 1, POS, 128), BF16),
             pltpu.VMEM((2, CROPS, PEERS, POS, 128), BF16),
             pltpu.VMEM((2, CROPS, 9, PEERS * POS, HALF), BF16),
-            pltpu.VMEM((2, 9, 128, HALF), F32),
-            pltpu.VMEM((6, OUT_SHARE, 768), BF16),
-            pltpu.VMEM((CHIPS, 3, OUT_SHARE, 128), BF16),
-            pltpu.VMEM((CHIPS - 1, 3, OUT_SHARE, 128), BF16),
+            pltpu.VMEM((2, 9, OUT_SHARE, HALF), F32),
+            pltpu.VMEM((3, 2, OUT_SHARE, 768), BF16),
+            pltpu.VMEM((3, CHIPS, OUT_SHARE, 128), BF16),
+            pltpu.VMEM((3, CHIPS - 1, OUT_SHARE, 128), BF16),
             pltpu.VMEM((C, 2 * HALF), BF16),
             pltpu.VMEM((C, 512), BF16),
             pltpu.VMEM((768, 512), BF16),
@@ -522,8 +581,12 @@
             dma((2, CROPS)),
             dma((2, CROPS)),
             dma((2, CROPS)),
-            dma,
-            dma,
+            dma((2, CROPS)),
+            dma((2, CROPS)),
+            dma((2, CROPS)),
+            dma((2, CROPS)),
+            dma((3,)),
+            dma((3,)),
         ],
         compiler_params=pltpu.CompilerParams(
             collective_id=0, has_side_effects=True, vmem_limit_bytes=60 * 1024 * 1024

time: 96.1 us -> 80.2 us (0.83)
  the two profiles are of different devices: /device:TPU:6 before, /device:TPU:1 now
where the time goes in v2:
time: 80.2 us; the launch traced here: 80 us
  Pallas kernels  76.1 us (95%)
  local copies, waits for them, and re-layouts  3.33 us (4%)
    pallas_call x1, Pallas kernels, shards(): pl.pallas_call(lambda *refs: kernel(scaling, *refs), out_shape=(jax.Shape...  76.1 us
    unnamed x2, local copies, waits for them, and re-layouts  3.33 us

profile of v2, /device:TPU:1, one launch (start us, length us, event | category | flops | bytes accessed | tf_op | source)
XLA Modules:
  0.0 80.0 jit_solution(10751034941995828282)
XLA Ops:
  0.6 76.1 %residual_step.1 = (f32[2,9,20,80]{3,2,1,0:T(8,128)}, bf16[4,64,320]{2,1,0:T(8,128)(2,1)}) custom-call(bf16[4,64,320]{2,1,0:T(8,128)(2,1)} %bitcast.7, bf16[2,9,320,320]{3,2,1,0:T(8,128)(2,1)} %bitcast.5, bf16[4,64,320]{2,1,0:T(8,128)(2,1)} %bitcast.8), custom_call_target="tpu_custom_call" | custom-call | tf_op jit(solution)/shard_map/residual_step/pallas_call | solution.py:540
  76.7 1.7 %copy.5 = f32[1,2,9,20,80]{4,1,3,2,0:T(2,128)} copy(f32[1,2,9,20,80]{4,3,2,1,0:T(8,128)} %bitcast.6) | data formatting | bytes 230400
  78.4 1.6 %copy.7 = bf16[1,1,4,8,8,320]{5,4,3,2,1,0:T(8,128)(2,1)} copy(bf16[1,1,4,8,8,320]{5,4,3,2,1,0:T(8,128)(2,1)} %bitcast.9) | data formatting | bytes 327680

commit v3 on v2

--- a/solution.py
+++ b/solution.py
@@ -296,6 +296,8 @@
         ((row < 8) & (slab == 0)) | ((row >= WIDE - 8) & (slab == SLABS - 1))
     )
 
+    last = CROPS - 1
+
     def share_field(a, k, wide):
         raw[a, k, IMAGES - 1] = wide
         for d in range(1, IMAGES):
@@ -324,8 +326,7 @@
                 device_id_type=MESH,
             ).start()
 
-    def share_grad(a, k, grad):
-        chunks = permuted(grad, sel[...])
+    def share_grad(a, k, chunks):
         gg[a, k, IMAGES - 1] = chunks[:, :128]
         for d in range(1, IMAGES):
             gs[a, k, d - 1] = chunks[:, 128 * d : 128 * (d + 1)]
@@ -349,7 +350,7 @@
             device_id_type=MESH,
         ).start()
 
-    def forward(k, carry):
+    def forward(k):
         arrive(fin, fr, k, s > 0)
         x = fin[k].astype(F32)
         hidden = conv(x, w, 0, WIDE)
@@ -364,21 +365,27 @@
 
         share_field(0, k, x[8 : 8 + WIDE].astype(BF16))
         share_field(1, k, active)
-        return carry
-
-    lax.fori_loop(0, CROPS, forward, 0)
-    pl.when(s == 0)(transpose_weights)
+
+        @pl.when((s == 0) & (k == last))
+        def _():
+            transpose_weights()
 
     def backward(k):
         arrive(gin, br, k, s < SECTIONS - 1)
         g = gin[k].astype(F32)
+        center = g[16 : 16 + POS]
+        ahead = (s == 0) & (k == last)
+
+        @pl.when(ahead)
+        def _():
+            share_grad(1, k, permuted(center.astype(BF16), sel[...]))
+
         grad_active = conv(g, wt, 1, WIDE)
         hidden = hid[k]
         q = sigmoid(hidden)
         slope = q * (1.0 + hidden * (1.0 - q))
         grad_hidden = jnp.where(inside, grad_active * slope, 0.0).astype(BF16)
         wide = grad_hidden.astype(F32)
-        center = g[16 : 16 + POS]
         grad_in = (center + conv(wide, wt, 0, POS)).astype(BF16)
         gout[k] = grad_in
 
@@ -388,8 +395,13 @@
 
         gi[k] = permuted(swap, grad_in)
         pltpu.make_async_copy(gi.at[k], gi_out.at[k], gi_sem.at[k]).start()
-        share_grad(1, k, center.astype(BF16))
-        share_grad(0, k, wide[8 : 8 + POS].astype(BF16))
+        lower = wide[8 : 8 + POS].astype(BF16)
+        chunks = permuted(jnp.concatenate([lower, center.astype(BF16)], axis=0), sel[...])
+        share_grad(0, k, chunks[:POS])
+
+        @pl.when(jnp.logical_not(ahead))
+        def _():
+            share_grad(1, k, chunks[POS:])
 
     def unfold(k):
         for a in range(2):
@@ -412,8 +424,6 @@
         for t in range(9):
             acc[a, t] += jnp.dot(grads, cc[a, k, t], preferred_element_type=F32)
 
-    early = s < 2
-
     def unfold_step(n):
         @pl.when(n < CROPS)
         def _():
@@ -423,20 +433,31 @@
         def _():
             unfold(n - 1)
 
-    def middle(i, carry):
-        unfolding = jnp.where(early, i <= CROPS, i >= CROPS)
-
-        @pl.when(unfolding)
-        def _():
-            unfold_step(jnp.where(early, i, i - CROPS))
-
-        @pl.when(jnp.logical_not(unfolding))
-        def _():
-            backward(jnp.where(early, i - CROPS - 1, i))
+    at_end = s == SECTIONS - 1
+    ahead_count = jnp.where(s == 0, CROPS + 1, jnp.where(s == 1, CROPS - 1, 0))
+
+    def step(i, carry):
+        back_from = CROPS + ahead_count
+        is_forward = jnp.where(at_end, (i < 2 * CROPS) & (i % 2 == 0), i < CROPS)
+        is_backward = jnp.where(
+            at_end, (i < 2 * CROPS) & (i % 2 == 1), (i >= back_from) & (i < back_from + CROPS)
+        )
+
+        @pl.when(is_forward)
+        def _():
+            forward(jnp.where(at_end, i // 2, i))
+
+        @pl.when(is_backward)
+        def _():
+            backward(jnp.where(at_end, i // 2, i - back_from))
+
+        @pl.when(jnp.logical_not(is_forward | is_backward))
+        def _():
+            unfold_step(jnp.where(i < back_from, i - CROPS, i - 2 * CROPS))
 
         return carry
 
-    lax.fori_loop(0, 2 * CROPS + 1, middle, 0)
+    lax.fori_loop(0, 3 * CROPS + 1, step, 0)
 
     def pack(t):
         for p in range(6):
@@ -448,7 +469,7 @@
         for half in range(2):
             for q in range(4):
                 pk[t, 4 * half + q] = packed[half, :, 128 * q : 128 * (q + 1)]
-        for d in range(1, CHIPS):
+        for d in (4, 3, 5, 2, 6, 1, 7):
             pltpu.make_async_remote_copy(
                 src_ref=pk.at[t, (z + d) % CHIPS],
                 dst_ref=rz.at[t, d - 1],
@@ -457,8 +478,6 @@
                 device_id=chip_of(d),
                 device_id_type=MESH,
             ).start()
-
-    last = CROPS - 1
 
     def hand_over(k, carry):
         relay_grad(1, k)

time: 80.2 us -> 79.3 us (0.989)
  the two profiles are of different devices: /device:TPU:1 before, /device:TPU:6 now
where the time goes in v3:
time: 79.3 us; the launch traced here: 79.2 us
  Pallas kernels  75.2 us (95%)
  local copies, waits for them, and re-layouts  3.33 us (4%)
    pallas_call x1, Pallas kernels, shards(): pl.pallas_call(lambda *refs: kernel(scaling, *refs), out_shape=(jax.Shape...  75.2 us
    unnamed x2, local copies, waits for them, and re-layouts  3.33 us

profile of v3, /device:TPU:6, one launch (start us, length us, event | category | flops | bytes accessed | tf_op | source)
XLA Modules:
  0.0 79.2 jit_solution(3539141629203105901)
XLA Ops:
  0.6 75.2 %residual_step.1 = (f32[2,9,20,80]{3,2,1,0:T(8,128)}, bf16[4,64,320]{2,1,0:T(8,128)(2,1)}) custom-call(bf16[4,64,320]{2,1,0:T(8,128)(2,1)} %bitcast.7, bf16[2,9,320,320]{3,2,1,0:T(8,128)(2,1)} %bitcast.5, bf16[4,64,320]{2,1,0:T(8,128)(2,1)} %bitcast.8), custom_call_target="tpu_custom_call" | custom-call | tf_op jit(solution)/shard_map/residual_step/pallas_call | solution.py:559
  75.9 1.7 %copy.5 = f32[1,2,9,20,80]{4,1,3,2,0:T(2,128)} copy(f32[1,2,9,20,80]{4,3,2,1,0:T(8,128)} %bitcast.6) | data formatting | bytes 230400
  77.6 1.6 %copy.7 = bf16[1,1,4,8,8,320]{5,4,3,2,1,0:T(8,128)(2,1)} copy(bf16[1,1,4,8,8,320]{5,4,3,2,1,0:T(8,128)(2,1)} %bitcast.9) | data formatting | bytes 327680

commit v4 on v3

--- a/solution.py
+++ b/solution.py
@@ -26,6 +26,7 @@
 IN_SHARE = C // SLABS
 HALF = 256
 PEERS = 8
+PAIR = 640
 
 
 def iota(shape, dim):
@@ -87,6 +88,7 @@
     pk,
     rz,
     pc,
+    pct,
     sel,
     c6,
     local_sem,
@@ -172,10 +174,17 @@
         greet(chip_of(d))
     i, j = iota((POS, POS), 0), iota((POS, POS), 1)
     swap = onehot((i // 8 == j % 8) & (i % 8 == j // 8))
-    i, j = iota((C, 2 * HALF), 0), iota((C, 2 * HALF), 1)
-    lane = j % 32
-    side = (j // HALF + core) % 2
-    pc[...] = onehot((lane < IN_SHARE) & (i == IN_SHARE * (2 * ((j % HALF) // 32) + side) + lane))
+    def chosen(first, shape):
+        i, j = iota(shape, 0) + first, iota(shape, 1)
+        lane = j % 32
+        side = (j // HALF + core) % 2
+        return (lane < IN_SHARE) & (i == IN_SHARE * (2 * ((j % HALF) // 32) + side) + lane)
+
+    pc[...] = onehot(chosen(0, (256, 2 * HALF)))
+    tail_row = iota((128, 2 * HALF), 0)
+    pct[0] = onehot(chosen(256, (128, 2 * HALF)) & (tail_row < 64))
+    pct[1] = onehot(chosen(192, (128, 2 * HALF)) & (tail_row >= 64))
+    i, j = iota((C, 512), 0), iota((C, 512), 1)
     lane = j % 128
     owner = (j // 128 + img) % IMAGES
     sel[...] = onehot((lane < OUT_SHARE) & (i == OUT_SHARE * owner + lane))
@@ -298,23 +307,30 @@
 
     last = CROPS - 1
 
-    def share_field(a, k, wide):
-        raw[a, k, IMAGES - 1] = wide
+    def share_fields(k, wide, active):
+        mine = raw.at[k, IMAGES - 1]
+        mine[:, 0:256] = wide[:, 0:256].astype(BF16)
+        mine[:, 256:512] = active[:, 0:256]
+        tails = jnp.concatenate([wide[:, 256:C], active[:, 256:C].astype(F32)], axis=1)
+        mine[:, 512:PAIR] = tails.astype(BF16)
         for d in range(1, IMAGES):
             pltpu.make_async_remote_copy(
-                src_ref=raw.at[a, k, IMAGES - 1],
-                dst_ref=raw.at[a, k, d - 1],
-                send_sem=raw_send.at[a, k],
-                recv_sem=raw_recv.at[a, k],
+                src_ref=mine,
+                dst_ref=raw.at[k, d - 1],
+                send_sem=raw_send.at[k],
+                recv_sem=raw_recv.at[k],
                 device_id=image_of(d),
                 device_id_type=MESH,
             ).start()
 
     def relay_field(k):
+        waited(raw.at[k, pl.ds(0, IMAGES - 1)], raw_recv.at[k])
         for a in range(2):
-            waited(raw.at[a, k, pl.ds(0, IMAGES - 1)], raw_recv.at[a, k])
             for n in range(IMAGES):
-                both = permuted(raw[a, k, n], pc[...])
+                both = (
+                    jnp.dot(raw[k, n, :, 256 * a : 256 * (a + 1)], pc[...], preferred_element_type=F32)
+                    + jnp.dot(raw[k, n, :, 512:PAIR], pct[a], preferred_element_type=F32)
+                ).astype(BF16)
                 fg[a, k, n] = both[:, :HALF]
                 fs[a, k, n] = both[:, HALF:]
             pltpu.make_async_remote_copy(
@@ -363,8 +379,7 @@
             fout[k] = result.astype(BF16)
             spread(fout, fin, fsend, fr, k, 1, True)
 
-        share_field(0, k, x[8 : 8 + WIDE].astype(BF16))
-        share_field(1, k, active)
+        share_fields(k, x[8 : 8 + WIDE], active)
 
         @pl.when((s == 0) & (k == last))
         def _():
@@ -403,6 +418,11 @@
         def _():
             share_grad(1, k, chunks[POS:])
 
+        @pl.when((s == 0) & (k >= 2))
+        def _():
+            relay_grad(1, k - 2)
+            relay_grad(0, k - 2)
+
     def unfold(k):
         for a in range(2):
             waited(fg.at[a, k, pl.ds(IMAGES, IMAGES)], fg_recv.at[a, k])
@@ -433,8 +453,21 @@
         def _():
             unfold(n - 1)
 
+            @pl.when(s > 0)
+            def _():
+                relay_grad(1, n - 1)
+                relay_grad(0, n - 1)
+
+        @pl.when((s > 0) & (n > 1))
+        def _():
+            def each(a, carry):
+                contract(a, n - 2)
+                return carry
+
+            lax.fori_loop(0, 2, each, 0)
+
     at_end = s == SECTIONS - 1
-    ahead_count = jnp.where(s == 0, CROPS + 1, jnp.where(s == 1, CROPS - 1, 0))
+    ahead_count = jnp.where(s == 0, CROPS + 1, 0)
 
     def step(i, carry):
         back_from = CROPS + ahead_count
@@ -479,33 +512,36 @@
                 device_id_type=MESH,
             ).start()
 
-    def hand_over(k, carry):
-        relay_grad(1, k)
-        relay_grad(0, k)
+    def tail(i, carry):
+        first = s == 0
+
+        @pl.when(first & (i == 2))
+        def _():
+            relay_grad(1, 2)
+            relay_grad(0, 2)
+
+        @pl.when(first & (i == 4))
+        def _():
+            relay_grad(1, last)
+
+        @pl.when(first & (i == 6))
+        def _():
+            relay_grad(0, last)
+
+        upper = ((i < 4) & (i % 2 == 0)) | (i == 4) | (i == 5)
+        crop = jnp.where(i < 4, i // 2, jnp.where(i % 2 == 0, 2, last))
+
+        @pl.when(first | (i != 6))
+        def _():
+            contract(jnp.where(upper, 1, 0), crop)
+
+        @pl.when(i == 5)
+        def _():
+            pack(2)
+
         return carry
 
-    lax.fori_loop(0, last, hand_over, 0)
-
-    def tail(i, carry):
-        @pl.when(i == 3)
-        def _():
-            relay_grad(1, last)
-
-        @pl.when(i == 4)
-        def _():
-            relay_grad(0, last)
-
-        upper = (i < 3) | (i == 5)
-        crop = jnp.where(i < 3, i, jnp.where(i < 5, i - 3, jnp.where(i == 5, last, i - 4)))
-        contract(jnp.where(upper, 1, 0), crop)
-
-        @pl.when(i == 5)
-        def _():
-            pack(2)
-
-        return carry
-
-    lax.fori_loop(0, 2 * CROPS, tail, 0)
+    lax.fori_loop(jnp.where(s == 0, 0, 5), 2 * CROPS, tail, 0)
     pack(1)
     pack(0)
 
@@ -514,10 +550,7 @@
         total = pk[t, z].astype(F32)
         for d in range(CHIPS - 1):
             total = total + rz[t, d].astype(F32)
-        flipped = (total * scaling).T
-        for p in range(6):
-            a, tap = divmod(6 * t + p, 9)
-            gk_out[a, tap] = flipped[IN_SHARE * p : IN_SHARE * (p + 1)]
+        gk_out[t] = (total * scaling).T
 
     for t in range(3):
         waited(rz.at[t], z_send.at[t])
@@ -541,14 +574,22 @@
         def _():
             sent(gout, bsend, k, True)
 
+        waited(raw.at[k, pl.ds(0, IMAGES - 1)], raw_send.at[k])
         for a in range(2):
-            waited(raw.at[a, k, pl.ds(0, IMAGES - 1)], raw_send.at[a, k])
             waited(fs.at[a, k], fg_send.at[a, k])
             waited(gs.at[a, k], gg_send.at[a, k])
             waited(gg.at[a, k, pl.ds(0, IMAGES)], gr_send.at[a, k])
         return carry
 
     lax.fori_loop(0, CROPS, drain, 0)
+
+
+def placed(gk, gi, gk_out, gi_out):
+    gi_out[...] = gi[...]
+    for n in range(18):
+        a, tap = divmod(n, 9)
+        t, p = divmod(n, 6)
+        gk_out[tap, :, a, :] = gk[t, IN_SHARE * p : IN_SHARE * (p + 1), :]
 
 
 def shards(strips, kernels, cotangent):
@@ -559,7 +600,7 @@
     gk, gi = pl.pallas_call(
         lambda *refs: kernel(scaling, *refs),
         out_shape=(
-            jax.ShapeDtypeStruct((2, 9, IN_SHARE, OUT_SHARE), F32),
+            jax.ShapeDtypeStruct((3, 128, OUT_SHARE), F32),
             jax.ShapeDtypeStruct((CROPS, POS, C), BF16),
         ),
         in_specs=[hbm, hbm, hbm],
@@ -575,7 +616,7 @@
             pltpu.VMEM((CROPS, POS, C), BF16),
             pltpu.VMEM((CROPS, POS, C), BF16),
             pltpu.VMEM((CROPS, WIDE, C), F32),
-            pltpu.VMEM((2, CROPS, IMAGES, WIDE, C), BF16),
+            pltpu.VMEM((CROPS, IMAGES, WIDE, PAIR), BF16),
             pltpu.VMEM((2, CROPS, IMAGES, WIDE, HALF), BF16),
             pltpu.VMEM((2, CROPS, PEERS, WIDE, HALF), BF16),
             pltpu.VMEM((2, CROPS, IMAGES - 1, POS, 128), BF16),
@@ -585,7 +626,8 @@
             pltpu.VMEM((3, 2, OUT_SHARE, 768), BF16),
             pltpu.VMEM((3, CHIPS, OUT_SHARE, 128), BF16),
             pltpu.VMEM((3, CHIPS - 1, OUT_SHARE, 128), BF16),
-            pltpu.VMEM((C, 2 * HALF), BF16),
+            pltpu.VMEM((256, 2 * HALF), BF16),
+            pltpu.VMEM((2, 128, 2 * HALF), BF16),
             pltpu.VMEM((C, 512), BF16),
             pltpu.VMEM((768, 512), BF16),
             dma((2,)),
@@ -596,8 +638,8 @@
             dma((CROPS, 3)),
             dma((CROPS, 3)),
             dma((CROPS, 3)),
-            dma((2, CROPS)),
-            dma((2, CROPS)),
+            dma((CROPS,)),
+            dma((CROPS,)),
             dma((2, CROPS)),
             dma((2, CROPS)),
             dma((2, CROPS)),
@@ -616,7 +658,17 @@
         kernels.reshape(2, 9, C, C),
         cotangent.reshape(CROPS, POS, C),
     )
-    return gk[None], gi.reshape(1, 1, CROPS, ROWS, COLS, C)
+    gk, gi = pl.pallas_call(
+        placed,
+        out_shape=(
+            jax.ShapeDtypeStruct((9, IN_SHARE, 2, OUT_SHARE), F32),
+            jax.ShapeDtypeStruct((CROPS, POS, C), BF16),
+        ),
+        in_specs=[vmem, vmem],
+        out_specs=(vmem, vmem),
+        name="outputs",
+    )(gk, gi)
+    return jnp.transpose(gk, (2, 0, 1, 3))[None], gi.reshape(1, 1, CROPS, ROWS, COLS, C)
 
 
 def solution(mesh):

time: 79.3 us -> 72.7 us (0.917)
  the two profiles are of different devices: /device:TPU:6 before, /device:TPU:1 now
where the time goes in v4:
time: 72.7 us; the launch traced here: 72.6 us
  Pallas kernels  71.9 us (99%)
    pallas_call x1, Pallas kernels, shards(): pl.pallas_call(lambda *refs: kernel(scaling, *refs), out_shape=(jax.Shape...  70.1 us
    pallas_call x1, Pallas kernels, shards(): pl.pallas_call(placed, out_shape=(jax.ShapeDtypeStruct((9, IN_SHARE, 2, O...  1.82 us

profile of v4, /device:TPU:1, one launch (start us, length us, event | category | flops | bytes accessed | tf_op | source)
XLA Modules:
  0.0 72.6 jit_solution(14648279208411113292)
XLA Ops:
  0.6 70.1 %residual_step.1 = (f32[3,128,80]{2,1,0:T(8,128)}, bf16[4,64,320]{2,1,0:T(8,128)(2,1)}) custom-call(bf16[4,64,320]{2,1,0:T(8,128)(2,1)} %bitcast.8, bf16[2,9,320,320]{3,2,1,0:T(8,128)(2,1)} %bitcast.7, bf16[4,64,320]{2,1,0:T(8,128)(2,1)} %bitcast.9), custom_call_target="tpu_custom_call" | custom-call | tf_op jit(solution)/shard_map/residual_step/pallas_call | solution.py:600
  70.7 1.8 %outputs.1 = (f32[9,20,2,80]{3,2,1,0:T(2,128)}, bf16[4,64,320]{2,1,0:T(8,128)(2,1)}) custom-call(f32[3,128,80]{2,1,0:T(8,128)} %get-tuple-element.6.gk, bf16[4,64,320]{2,1,0:T(8,128)(2,1)} %get-tuple-element.7.gi), custom_call_target="tpu_custom_call" | custom-call | tf_op jit(solution)/shard_map/outputs/pallas_call | solution.py:661

commit v5 on v4

--- a/solution.py
+++ b/solution.py
@@ -71,7 +71,6 @@
     wt,
     sv,
     cv,
-    gi,
     fin,
     gin,
     fout,
@@ -93,7 +92,6 @@
     c6,
     local_sem,
     weight_sem,
-    gi_sem,
     fr,
     fsend,
     br,
@@ -269,6 +267,19 @@
     loads[0].wait()
     loads[1].wait()
 
+    def share_grad(a, k, chunks):
+        gg[a, k, IMAGES - 1] = chunks[:, :128]
+        for d in range(1, IMAGES):
+            gs[a, k, d - 1] = chunks[:, 128 * d : 128 * (d + 1)]
+            pltpu.make_async_remote_copy(
+                src_ref=gs.at[a, k, d - 1],
+                dst_ref=gg.at[a, k, d - 1],
+                send_sem=gg_send.at[a, k],
+                recv_sem=gg_recv.at[a, k],
+                device_id=image_of(d),
+                device_id_type=MESH,
+            ).start()
+
     @pl.when(s == 0)
     def _():
         def step(k, carry):
@@ -281,8 +292,10 @@
     @pl.when(s == SECTIONS - 1)
     def _():
         def step(k, carry):
-            gin[k, 16 : 16 + POS, :] = permuted(swap, cv[k])
+            center = permuted(swap, cv[k])
+            gin[k, 16 : 16 + POS, :] = center
             spread(gin, gin, edge_send, br, k, 0, False)
+            share_grad(1, k, permuted(center, sel[...]))
             return carry
 
         lax.fori_loop(0, CROPS, step, 0)
@@ -342,19 +355,6 @@
                 device_id_type=MESH,
             ).start()
 
-    def share_grad(a, k, chunks):
-        gg[a, k, IMAGES - 1] = chunks[:, :128]
-        for d in range(1, IMAGES):
-            gs[a, k, d - 1] = chunks[:, 128 * d : 128 * (d + 1)]
-            pltpu.make_async_remote_copy(
-                src_ref=gs.at[a, k, d - 1],
-                dst_ref=gg.at[a, k, d - 1],
-                send_sem=gg_send.at[a, k],
-                recv_sem=gg_recv.at[a, k],
-                device_id=image_of(d),
-                device_id_type=MESH,
-            ).start()
-
     def relay_grad(a, k):
         waited(gg.at[a, k, pl.ds(0, IMAGES - 1)], gg_recv.at[a, k])
         pltpu.make_async_remote_copy(
@@ -389,9 +389,10 @@
         arrive(gin, br, k, s < SECTIONS - 1)
         g = gin[k].astype(F32)
         center = g[16 : 16 + POS]
-        ahead = (s == 0) & (k == last)
-
-        @pl.when(ahead)
+        at_last = (s == 0) & (k == last)
+        shared = at_last | (s == SECTIONS - 1)
+
+        @pl.when(at_last)
         def _():
             share_grad(1, k, permuted(center.astype(BF16), sel[...]))
 
@@ -408,13 +409,12 @@
         def _():
             spread(gout, gin, bsend, br, k, -1, True)
 
-        gi[k] = permuted(swap, grad_in)
-        pltpu.make_async_copy(gi.at[k], gi_out.at[k], gi_sem.at[k]).start()
+        gi_out[k] = permuted(swap, grad_in)
         lower = wide[8 : 8 + POS].astype(BF16)
         chunks = permuted(jnp.concatenate([lower, center.astype(BF16)], axis=0), sel[...])
         share_grad(0, k, chunks[:POS])
 
-        @pl.when(jnp.logical_not(ahead))
+        @pl.when(jnp.logical_not(shared))
         def _():
             share_grad(1, k, chunks[POS:])
 
@@ -444,21 +444,12 @@
         for t in range(9):
             acc[a, t] += jnp.dot(grads, cc[a, k, t], preferred_element_type=F32)
 
-    def unfold_step(n):
-        @pl.when(n < CROPS)
-        def _():
-            relay_field(n)
-
-        @pl.when(n > 0)
-        def _():
-            unfold(n - 1)
-
-            @pl.when(s > 0)
-            def _():
-                relay_grad(1, n - 1)
-                relay_grad(0, n - 1)
-
-        @pl.when((s > 0) & (n > 1))
+    ahead_count = jnp.where(s == 0, CROPS + 1, jnp.where(s == 1, CROPS - 1, 0))
+
+    def unfold_step(n, early):
+        late = jnp.logical_not(early)
+
+        @pl.when(late & (n > 1))
         def _():
             def each(a, carry):
                 contract(a, n - 2)
@@ -466,8 +457,22 @@
 
             lax.fori_loop(0, 2, each, 0)
 
+        todo = early | (n >= ahead_count)
+
+        @pl.when(todo & (n > 0))
+        def _():
+            unfold(n - 1)
+
+        @pl.when(late & (n > 0))
+        def _():
+            relay_grad(1, n - 1)
+            relay_grad(0, n - 1)
+
+        @pl.when(todo & (n < CROPS))
+        def _():
+            relay_field(n)
+
     at_end = s == SECTIONS - 1
-    ahead_count = jnp.where(s == 0, CROPS + 1, 0)
 
     def step(i, carry):
         back_from = CROPS + ahead_count
@@ -486,11 +491,12 @@
 
         @pl.when(jnp.logical_not(is_forward | is_backward))
         def _():
-            unfold_step(jnp.where(i < back_from, i - CROPS, i - 2 * CROPS))
+            early = i < back_from
+            unfold_step(jnp.where(early, i - CROPS, i - back_from - CROPS), early)
 
         return carry
 
-    lax.fori_loop(0, 3 * CROPS + 1, step, 0)
+    lax.fori_loop(0, 3 * CROPS + 1 + jnp.where(s == 1, ahead_count, 0), step, 0)
 
     def pack(t):
         for p in range(6):
@@ -556,8 +562,6 @@
         waited(rz.at[t], z_send.at[t])
 
     def drain(k, carry):
-        pltpu.make_async_copy(gi.at[k], gi_out.at[k], gi_sem.at[k]).wait()
-
         @pl.when(s == 0)
         def _():
             sent(fin, edge_send, k, None)
@@ -600,15 +604,14 @@
     gk, gi = pl.pallas_call(
         lambda *refs: kernel(scaling, *refs),
         out_shape=(
-            jax.ShapeDtypeStruct((3, 128, OUT_SHARE), F32),
-            jax.ShapeDtypeStruct((CROPS, POS, C), BF16),
+            pltpu.VMEM((3, 128, OUT_SHARE), F32),
+            pltpu.VMEM((CROPS, POS, C), BF16),
         ),
         in_specs=[hbm, hbm, hbm],
-        out_specs=(vmem, hbm),
+        out_specs=(vmem, vmem),
         scratch_shapes=[
             pltpu.VMEM((2, 9, C, C), BF16),
             pltpu.VMEM((2, 9, C, C), BF16),
-            pltpu.VMEM((CROPS, POS, C), BF16),
             pltpu.VMEM((CROPS, POS, C), BF16),
             pltpu.VMEM((CROPS, POS, C), BF16),
             pltpu.VMEM((CROPS, DEEP, C), BF16),
@@ -632,7 +635,6 @@
             pltpu.VMEM((768, 512), BF16),
             dma((2,)),
             dma((2, 9)),
-            dma((CROPS,)),
             dma((CROPS, 3)),
             dma((CROPS, 3)),
             dma((CROPS, 3)),
@@ -667,7 +669,10 @@
         in_specs=[vmem, vmem],
         out_specs=(vmem, vmem),
         name="outputs",
-    )(gk, gi)
+    )(
+        pltpu.with_memory_space_constraint(gk, pltpu.VMEM),
+        pltpu.with_memory_space_constraint(gi, pltpu.VMEM),
+    )
     return jnp.transpose(gk, (2, 0, 1, 3))[None], gi.reshape(1, 1, CROPS, ROWS, COLS, C)
 
 

time: 72.7 us -> 71.5 us (0.983)
  Pallas kernels: 71.9 us -> 70.8 us
    pallas_call x1, Pallas kernels: 1.82 us -> 0.79 us  [shards(): pl.pallas_call(placed, out_shape=(jax.ShapeDtypeStruct((9, IN_SHARE, 2, O...]
where the time goes in v5:
time: 71.5 us; the launch traced here: 71.4 us
  Pallas kernels  70.8 us (99%)
    pallas_call x1, Pallas kernels, shards(): pl.pallas_call(lambda *refs: kernel(scaling, *refs), out_shape=(pltpu.VME...  70 us

profile of v5, /device:TPU:1, one launch (start us, length us, event | category | flops | bytes accessed | tf_op | source)
XLA Modules:
  0.0 71.4 jit_solution(2911025735579202684)
XLA Ops:
  0.6 70.0 %residual_step.1 = (f32[3,128,80]{2,1,0:T(8,128)S(1)}, bf16[4,64,320]{2,1,0:T(8,128)(2,1)S(1)}) custom-call(bf16[4,64,320]{2,1,0:T(8,128)(2,1)} %bitcast.8, bf16[2,9,320,320]{3,2,1,0:T(8,128)(2,1)} %bitcast.7, bf16[4,64,320]{2,1,0:T(8,128)(2,1)} %bitcast.9), custom_call_target="tpu_custom_call" | custom-call | tf_op jit(solution)/shard_map/residual_step/pallas_call | solution.py:604
  70.6 0.8 %outputs.1 = (f32[9,20,2,80]{3,2,1,0:T(2,128)}, bf16[4,64,320]{2,1,0:T(8,128)(2,1)}) custom-call(f32[3,128,80]{2,1,0:T(8,128)S(1)} %get-tuple-element.6.gk, bf16[4,64,320]{2,1,0:T(8,128)(2,1)S(1)} %get-tuple-element.7.gi), custom_call_target="tpu_custom_call" | custom-call | tf_op jit(solution)/shard_map/outputs/pallas_call | solution.py:663

commit v6 on v5

--- a/solution.py
+++ b/solution.py
@@ -107,6 +107,7 @@
     gr_send,
     z_recv,
     z_send,
+    token,
 ):
     s = lax.axis_index("section")
     slab = lax.axis_index("slab")
@@ -124,7 +125,7 @@
         for tap in range(9):
             loads.append(
                 pltpu.make_async_copy(
-                    kernels.at[part, tap], w.at[part, tap], weight_sem.at[part, tap]
+                    kernels.at[part, tap], w.at[part, tap], weight_sem
                 )
             )
     for load in loads:
@@ -168,7 +169,7 @@
     for d in range(1, IMAGES):
         greet(image_of(d))
     greet(partner)
-    for d in range(1, CHIPS):
+    for d in (1, CHIPS - 1):
         greet(chip_of(d))
     i, j = iota((POS, POS), 0), iota((POS, POS), 1)
     swap = onehot((i // 8 == j % 8) & (i % 8 == j // 8))
@@ -195,7 +196,7 @@
     )
 
     acc[...] = jnp.zeros_like(acc)
-    pl.semaphore_wait(barrier, greeted + IMAGES + (CHIPS - 1))
+    pl.semaphore_wait(barrier, greeted + IMAGES + 2)
 
     def permuted(x, matrix):
         return jnp.dot(x, matrix, preferred_element_type=F32).astype(BF16)
@@ -208,8 +209,8 @@
             pltpu.make_async_remote_copy(
                 src_ref=src.at[k, pl.ds(base + POS - 16, 16)],
                 dst_ref=dst.at[k, pl.ds(0, 16)],
-                send_sem=send.at[k, 2],
-                recv_sem=recv.at[k, 0],
+                send_sem=send.at[2],
+                recv_sem=recv.at[k],
                 device_id=(s + ds, slab + 1, img),
                 device_id_type=MESH,
             ).start()
@@ -219,8 +220,8 @@
             pltpu.make_async_remote_copy(
                 src_ref=src.at[k, pl.ds(base, 16)],
                 dst_ref=dst.at[k, pl.ds(DEEP - 16, 16)],
-                send_sem=send.at[k, 0],
-                recv_sem=recv.at[k, 2],
+                send_sem=send.at[0],
+                recv_sem=recv.at[k],
                 device_id=(s + ds, slab - 1, img),
                 device_id_type=MESH,
             ).start()
@@ -229,8 +230,8 @@
             pltpu.make_async_remote_copy(
                 src_ref=src.at[k],
                 dst_ref=dst.at[k, pl.ds(16, POS)],
-                send_sem=send.at[k, 1],
-                recv_sem=recv.at[k, 1],
+                send_sem=send.at[1],
+                recv_sem=recv.at[k],
                 device_id=(s + ds, slab, img),
                 device_id_type=MESH,
             ).start()
@@ -238,31 +239,32 @@
     def waited(ref, sem):
         pltpu.make_async_copy(ref, ref, sem).wait()
 
+    inner = has_left & has_right
+
     def arrive(dst, recv, k, center):
-        @pl.when(center)
-        def _():
-            waited(dst.at[k, pl.ds(16, POS)], recv.at[k, 1])
+        other = jnp.logical_not(center)
+        for case, rows in (
+            (center & inner, DEEP),
+            (center & jnp.logical_not(inner), DEEP - 16),
+            (other & inner, 32),
+            (other & jnp.logical_not(inner), 16),
+        ):
+
+            @pl.when(case)
+            def _():
+                waited(dst.at[k, pl.ds(0, rows)], recv.at[k])
+
+    def sent(src, send, center):
+        if center:
+            waited(src, send.at[1])
+
+        @pl.when(has_right)
+        def _():
+            waited(src.at[:, pl.ds(0, 16)], send.at[2])
 
         @pl.when(has_left)
         def _():
-            waited(dst.at[k, pl.ds(0, 16)], recv.at[k, 0])
-
-        @pl.when(has_right)
-        def _():
-            waited(dst.at[k, pl.ds(DEEP - 16, 16)], recv.at[k, 2])
-
-    def sent(src, send, k, center):
-        base = 16 if center is None else 0
-        if center is not None:
-            waited(src.at[k], send.at[k, 1])
-
-        @pl.when(has_right)
-        def _():
-            waited(src.at[k, pl.ds(base + POS - 16, 16)], send.at[k, 2])
-
-        @pl.when(has_left)
-        def _():
-            waited(src.at[k, pl.ds(base, 16)], send.at[k, 0])
+            waited(src.at[:, pl.ds(0, 16)], send.at[0])
 
     loads[0].wait()
     loads[1].wait()
@@ -274,7 +276,7 @@
             pltpu.make_async_remote_copy(
                 src_ref=gs.at[a, k, d - 1],
                 dst_ref=gg.at[a, k, d - 1],
-                send_sem=gg_send.at[a, k],
+                send_sem=gg_send,
                 recv_sem=gg_recv.at[a, k],
                 device_id=image_of(d),
                 device_id_type=MESH,
@@ -300,8 +302,7 @@
 
         lax.fori_loop(0, CROPS, step, 0)
 
-    for load in loads[2:]:
-        load.wait()
+    waited(w, weight_sem)
 
     def transpose_weights():
         def step(n, carry):
@@ -330,7 +331,7 @@
             pltpu.make_async_remote_copy(
                 src_ref=mine,
                 dst_ref=raw.at[k, d - 1],
-                send_sem=raw_send.at[k],
+                send_sem=raw_send,
                 recv_sem=raw_recv.at[k],
                 device_id=image_of(d),
                 device_id_type=MESH,
@@ -349,7 +350,7 @@
             pltpu.make_async_remote_copy(
                 src_ref=fs.at[a, k],
                 dst_ref=fg.at[a, k, pl.ds(IMAGES, IMAGES)],
-                send_sem=fg_send.at[a, k],
+                send_sem=fg_send,
                 recv_sem=fg_recv.at[a, k],
                 device_id=partner,
                 device_id_type=MESH,
@@ -360,7 +361,7 @@
         pltpu.make_async_remote_copy(
             src_ref=gg.at[a, k, pl.ds(0, IMAGES)],
             dst_ref=gg.at[a, k, pl.ds(IMAGES, IMAGES)],
-            send_sem=gr_send.at[a, k],
+            send_sem=gr_send,
             recv_sem=gr_recv.at[a, k],
             device_id=partner,
             device_id_type=MESH,
@@ -475,6 +476,19 @@
     at_end = s == SECTIONS - 1
 
     def step(i, carry):
+        turn = i - CROPS
+
+        @pl.when((turn > 0) & (turn <= 3))
+        def _():
+            pl.semaphore_wait(token.at[turn - 1], 2)
+
+        @pl.when((turn >= 0) & (turn < 3))
+        def _():
+            for d in (1, CHIPS - 1):
+                pl.semaphore_signal(
+                    token.at[turn], inc=1, device_id=chip_of(d), device_id_type=MESH
+                )
+
         back_from = CROPS + ahead_count
         is_forward = jnp.where(at_end, (i < 2 * CROPS) & (i % 2 == 0), i < CROPS)
         is_backward = jnp.where(
@@ -512,7 +526,7 @@
             pltpu.make_async_remote_copy(
                 src_ref=pk.at[t, (z + d) % CHIPS],
                 dst_ref=rz.at[t, d - 1],
-                send_sem=z_send.at[t],
+                send_sem=z_send,
                 recv_sem=z_recv.at[t],
                 device_id=chip_of(d),
                 device_id_type=MESH,
@@ -558,34 +572,27 @@
             total = total + rz[t, d].astype(F32)
         gk_out[t] = (total * scaling).T
 
-    for t in range(3):
-        waited(rz.at[t], z_send.at[t])
-
-    def drain(k, carry):
-        @pl.when(s == 0)
-        def _():
-            sent(fin, edge_send, k, None)
-
-        @pl.when(s == SECTIONS - 1)
-        def _():
-            sent(gin, edge_send, k, None)
-
-        @pl.when(s < SECTIONS - 1)
-        def _():
-            sent(fout, fsend, k, True)
-
-        @pl.when(s > 0)
-        def _():
-            sent(gout, bsend, k, True)
-
-        waited(raw.at[k, pl.ds(0, IMAGES - 1)], raw_send.at[k])
-        for a in range(2):
-            waited(fs.at[a, k], fg_send.at[a, k])
-            waited(gs.at[a, k], gg_send.at[a, k])
-            waited(gg.at[a, k, pl.ds(0, IMAGES)], gr_send.at[a, k])
-        return carry
-
-    lax.fori_loop(0, CROPS, drain, 0)
+    waited(rz, z_send)
+    waited(raw.at[:, pl.ds(0, IMAGES - 1)], raw_send)
+    waited(fs, fg_send)
+    waited(gs, gg_send)
+    waited(gg.at[:, :, pl.ds(0, IMAGES)], gr_send)
+
+    @pl.when(s == 0)
+    def _():
+        sent(fin, edge_send, False)
+
+    @pl.when(s == SECTIONS - 1)
+    def _():
+        sent(gin, edge_send, False)
+
+    @pl.when(s < SECTIONS - 1)
+    def _():
+        sent(fout, fsend, True)
+
+    @pl.when(s > 0)
+    def _():
+        sent(gout, bsend, True)
 
 
 def placed(gk, gi, gk_out, gi_out):
@@ -634,22 +641,23 @@
             pltpu.VMEM((C, 512), BF16),
             pltpu.VMEM((768, 512), BF16),
             dma((2,)),
-            dma((2, 9)),
-            dma((CROPS, 3)),
-            dma((CROPS, 3)),
-            dma((CROPS, 3)),
-            dma((CROPS, 3)),
-            dma((CROPS, 3)),
+            dma,
             dma((CROPS,)),
+            dma((3,)),
             dma((CROPS,)),
-            dma((2, CROPS)),
-            dma((2, CROPS)),
-            dma((2, CROPS)),
-            dma((2, CROPS)),
-            dma((2, CROPS)),
-            dma((2, CROPS)),
             dma((3,)),
             dma((3,)),
+            dma((CROPS,)),
+            dma,
+            dma((2, CROPS)),
+            dma,
+            dma((2, CROPS)),
+            dma,
+            dma((2, CROPS)),
+            dma,
+            dma((3,)),
+            dma,
+            pltpu.SemaphoreType.REGULAR((3,)),
         ],
         compiler_params=pltpu.CompilerParams(
             collective_id=0, has_side_effects=True, vmem_limit_bytes=60 * 1024 * 1024

time: 71.5 us -> 70.8 us (level)
  no operation moved by 1% of the time
where the time goes in v6:
time: 70.8 us; the launch traced here: 70.7 us
  Pallas kernels  70.1 us (99%)
    pallas_call x1, Pallas kernels, shards(): pl.pallas_call(lambda *refs: kernel(scaling, *refs), out_shape=(pltpu.VME...  69.3 us

profile of v6, /device:TPU:1, one launch (start us, length us, event | category | flops | bytes accessed | tf_op | source)
XLA Modules:
  0.0 70.7 jit_solution(12263555029572603454)
XLA Ops:
  0.6 69.3 %residual_step.1 = (f32[3,128,80]{2,1,0:T(8,128)S(1)}, bf16[4,64,320]{2,1,0:T(8,128)(2,1)S(1)}) custom-call(bf16[4,64,320]{2,1,0:T(8,128)(2,1)} %bitcast.8, bf16[2,9,320,320]{3,2,1,0:T(8,128)(2,1)} %bitcast.7, bf16[4,64,320]{2,1,0:T(8,128)(2,1)} %bitcast.9), custom_call_target="tpu_custom_call" | custom-call | tf_op jit(solution)/shard_map/residual_step/pallas_call | solution.py:611
  69.9 0.8 %outputs.1 = (f32[9,20,2,80]{3,2,1,0:T(2,128)}, bf16[4,64,320]{2,1,0:T(8,128)(2,1)}) custom-call(f32[3,128,80]{2,1,0:T(8,128)S(1)} %get-tuple-element.6.gk, bf16[4,64,320]{2,1,0:T(8,128)(2,1)S(1)} %get-tuple-element.7.gi), custom_call_target="tpu_custom_call" | custom-call | tf_op jit(solution)/shard_map/outputs/pallas_call | solution.py:671

commit v7 on v6

--- a/solution.py
+++ b/solution.py
@@ -80,6 +80,7 @@
     fs,
     fg,
     gs,
+    us,
     gg,
     cc,
     acc,
@@ -103,6 +104,7 @@
     fg_send,
     gg_recv,
     gg_send,
+    up_send,
     gr_recv,
     gr_send,
     z_recv,
@@ -276,7 +278,7 @@
             pltpu.make_async_remote_copy(
                 src_ref=gs.at[a, k, d - 1],
                 dst_ref=gg.at[a, k, d - 1],
-                send_sem=gg_send,
+                send_sem=gg_send.at[a],
                 recv_sem=gg_recv.at[a, k],
                 device_id=image_of(d),
                 device_id_type=MESH,
@@ -356,8 +358,8 @@
                 device_id_type=MESH,
             ).start()
 
-    def relay_grad(a, k):
-        waited(gg.at[a, k, pl.ds(0, IMAGES - 1)], gg_recv.at[a, k])
+    def relay_grad(a, k, slots=IMAGES - 1):
+        waited(gg.at[a, k, pl.ds(0, slots)], gg_recv.at[a, k])
         pltpu.make_async_remote_copy(
             src_ref=gg.at[a, k, pl.ds(0, IMAGES)],
             dst_ref=gg.at[a, k, pl.ds(IMAGES, IMAGES)],
@@ -390,13 +392,7 @@
         arrive(gin, br, k, s < SECTIONS - 1)
         g = gin[k].astype(F32)
         center = g[16 : 16 + POS]
-        at_last = (s == 0) & (k == last)
-        shared = at_last | (s == SECTIONS - 1)
-
-        @pl.when(at_last)
-        def _():
-            share_grad(1, k, permuted(center.astype(BF16), sel[...]))
-
+        shared = ((s == 0) & (k == last)) | (s == SECTIONS - 1)
         grad_active = conv(g, wt, 1, WIDE)
         hidden = hid[k]
         q = sigmoid(hidden)
@@ -410,6 +406,20 @@
         def _():
             spread(gout, gin, bsend, br, k, -1, True)
 
+        @pl.when((s == 1) & (k == last))
+        def _():
+            above = permuted(grad_in, sel[...])
+            for d in range(IMAGES):
+                us[d] = above[:, 128 * d : 128 * (d + 1)]
+                pltpu.make_async_remote_copy(
+                    src_ref=us.at[d],
+                    dst_ref=gg.at[1, k, (d + IMAGES - 1) % IMAGES],
+                    send_sem=up_send,
+                    recv_sem=gg_recv.at[1, k],
+                    device_id=(s - 1, slab, (img + d) % IMAGES),
+                    device_id_type=MESH,
+                ).start()
+
         gi_out[k] = permuted(swap, grad_in)
         lower = wide[8 : 8 + POS].astype(BF16)
         chunks = permuted(jnp.concatenate([lower, center.astype(BF16)], axis=0), sel[...])
@@ -476,7 +486,7 @@
     at_end = s == SECTIONS - 1
 
     def step(i, carry):
-        turn = i - CROPS
+        turn = i - jnp.where(s == 0, CROPS, 2 * CROPS + ahead_count)
 
         @pl.when((turn > 0) & (turn <= 3))
         def _():
@@ -542,7 +552,7 @@
 
         @pl.when(first & (i == 4))
         def _():
-            relay_grad(1, last)
+            relay_grad(1, last, IMAGES)
 
         @pl.when(first & (i == 6))
         def _():
@@ -575,7 +585,20 @@
     waited(rz, z_send)
     waited(raw.at[:, pl.ds(0, IMAGES - 1)], raw_send)
     waited(fs, fg_send)
-    waited(gs, gg_send)
+    waited(gs.at[0], gg_send.at[0])
+
+    @pl.when(s == 0)
+    def _():
+        waited(gs.at[1, pl.ds(0, last)], gg_send.at[1])
+
+    @pl.when(s > 0)
+    def _():
+        waited(gs.at[1], gg_send.at[1])
+
+    @pl.when(s == 1)
+    def _():
+        waited(us, up_send)
+
     waited(gg.at[:, :, pl.ds(0, IMAGES)], gr_send)
 
     @pl.when(s == 0)
@@ -630,6 +653,7 @@
             pltpu.VMEM((2, CROPS, IMAGES, WIDE, HALF), BF16),
             pltpu.VMEM((2, CROPS, PEERS, WIDE, HALF), BF16),
             pltpu.VMEM((2, CROPS, IMAGES - 1, POS, 128), BF16),
+            pltpu.VMEM((IMAGES, POS, 128), BF16),
             pltpu.VMEM((2, CROPS, PEERS, POS, 128), BF16),
             pltpu.VMEM((2, CROPS, 9, PEERS * POS, HALF), BF16),
             pltpu.VMEM((2, 9, OUT_SHARE, HALF), F32),
@@ -652,6 +676,7 @@
             dma((2, CROPS)),
             dma,
             dma((2, CROPS)),
+            dma((2,)),
             dma,
             dma((2, CROPS)),
             dma,

time: 70.8 us -> 69 us (0.975)
  Pallas kernels: 70.1 us -> 68.2 us
    pallas_call x1, Pallas kernels: 69.3 us -> 67.4 us  [shards(): pl.pallas_call(lambda *refs: kernel(scaling, *refs), out_shape=(pltpu.VME...]
where the time goes in v7:
time: 69 us; the launch traced here: 68.9 us
  Pallas kernels  68.2 us (99%)
    pallas_call x1, Pallas kernels, shards(): pl.pallas_call(lambda *refs: kernel(scaling, *refs), out_shape=(pltpu.VME...  67.4 us

profile of v7, /device:TPU:1, one launch (start us, length us, event | category | flops | bytes accessed | tf_op | source)
XLA Modules:
  0.0 68.9 jit_solution(10232688946553462664)
XLA Ops:
  0.6 67.4 %residual_step.1 = (f32[3,128,80]{2,1,0:T(8,128)S(1)}, bf16[4,64,320]{2,1,0:T(8,128)(2,1)S(1)}) custom-call(bf16[4,64,320]{2,1,0:T(8,128)(2,1)} %bitcast.8, bf16[2,9,320,320]{3,2,1,0:T(8,128)(2,1)} %bitcast.7, bf16[4,64,320]{2,1,0:T(8,128)(2,1)} %bitcast.9), custom_call_target="tpu_custom_call" | custom-call | tf_op jit(solution)/shard_map/residual_step/pallas_call | solution.py:634
  68.1 0.8 %outputs.1 = (f32[9,20,2,80]{3,2,1,0:T(2,128)}, bf16[4,64,320]{2,1,0:T(8,128)(2,1)}) custom-call(f32[3,128,80]{2,1,0:T(8,128)S(1)} %get-tuple-element.6.gk, bf16[4,64,320]{2,1,0:T(8,128)(2,1)S(1)} %get-tuple-element.7.gi), custom_call_target="tpu_custom_call" | custom-call | tf_op jit(solution)/shard_map/outputs/pallas_call | solution.py:696

commit v8 on v7

--- a/solution.py
+++ b/solution.py
@@ -26,6 +26,7 @@
 IN_SHARE = C // SLABS
 HALF = 256
 PEERS = 8
+DIRECT = (3, 5, 2, 6, 1, 7)
 PAIR = 640
 
 
@@ -87,6 +88,7 @@
     pkl,
     pk,
     rz,
+    far,
     pc,
     pct,
     sel,
@@ -108,6 +110,7 @@
     gr_recv,
     gr_send,
     z_recv,
+    far_recv,
     z_send,
     token,
 ):
@@ -429,7 +432,7 @@
         def _():
             share_grad(1, k, chunks[POS:])
 
-        @pl.when((s == 0) & (k >= 2))
+        @pl.when((s <= 1) & (k >= 2))
         def _():
             relay_grad(1, k - 2)
             relay_grad(0, k - 2)
@@ -474,7 +477,7 @@
         def _():
             unfold(n - 1)
 
-        @pl.when(late & (n > 0))
+        @pl.when(late & (n > jnp.where(s == 1, 2, 0)))
         def _():
             relay_grad(1, n - 1)
             relay_grad(0, n - 1)
@@ -521,6 +524,16 @@
         return carry
 
     lax.fori_loop(0, 3 * CROPS + 1 + jnp.where(s == 1, ahead_count, 0), step, 0)
+
+    def send_block(block, t, d, dst, recv):
+        pltpu.make_async_remote_copy(
+            src_ref=pk.at[t, block],
+            dst_ref=dst,
+            send_sem=z_send,
+            recv_sem=recv,
+            device_id=chip_of(d),
+            device_id_type=MESH,
+        ).start()
 
     def pack(t):
         for p in range(6):
@@ -532,15 +545,18 @@
         for half in range(2):
             for q in range(4):
                 pk[t, 4 * half + q] = packed[half, :, 128 * q : 128 * (q + 1)]
-        for d in (4, 3, 5, 2, 6, 1, 7):
-            pltpu.make_async_remote_copy(
-                src_ref=pk.at[t, (z + d) % CHIPS],
-                dst_ref=rz.at[t, d - 1],
-                send_sem=z_send,
-                recv_sem=z_recv.at[t],
-                device_id=chip_of(d),
-                device_id_type=MESH,
-            ).start()
+        near, held = (1, 3) if t % 2 == 0 else (7, 5)
+        send_block((z + 4) % CHIPS, t, near, far.at[t], far_recv.at[t])
+        for slot, d in enumerate(DIRECT):
+            if d != held:
+                send_block((z + d) % CHIPS, t, d, rz.at[t, slot], z_recv.at[t])
+
+    def merge(t):
+        held = 3 if t % 2 == 0 else 5
+        waited(far.at[t], far_recv.at[t])
+        mine = pk.at[t, (z + held) % CHIPS]
+        mine[...] = (mine[...].astype(F32) + far[t].astype(F32)).astype(BF16)
+        send_block((z + held) % CHIPS, t, held, rz.at[t, DIRECT.index(held)], z_recv.at[t])
 
     def tail(i, carry):
         first = s == 0
@@ -574,15 +590,18 @@
     lax.fori_loop(jnp.where(s == 0, 0, 5), 2 * CROPS, tail, 0)
     pack(1)
     pack(0)
+    merge(2)
+    merge(1)
+    merge(0)
 
     for t in (2, 1, 0):
         waited(rz.at[t], z_recv.at[t])
         total = pk[t, z].astype(F32)
-        for d in range(CHIPS - 1):
-            total = total + rz[t, d].astype(F32)
+        for slot in range(len(DIRECT)):
+            total = total + rz[t, slot].astype(F32)
         gk_out[t] = (total * scaling).T
 
-    waited(rz, z_send)
+    waited(pk.at[:, pl.ds(0, CHIPS - 1)], z_send)
     waited(raw.at[:, pl.ds(0, IMAGES - 1)], raw_send)
     waited(fs, fg_send)
     waited(gs.at[0], gg_send.at[0])
@@ -659,7 +678,8 @@
             pltpu.VMEM((2, 9, OUT_SHARE, HALF), F32),
             pltpu.VMEM((3, 2, OUT_SHARE, 768), BF16),
             pltpu.VMEM((3, CHIPS, OUT_SHARE, 128), BF16),
-            pltpu.VMEM((3, CHIPS - 1, OUT_SHARE, 128), BF16),
+            pltpu.VMEM((3, len(DIRECT), OUT_SHARE, 128), BF16),
+            pltpu.VMEM((3, OUT_SHARE, 128), BF16),
             pltpu.VMEM((256, 2 * HALF), BF16),
             pltpu.VMEM((2, 128, 2 * HALF), BF16),
             pltpu.VMEM((C, 512), BF16),
@@ -680,6 +700,7 @@
             dma,
             dma((2, CROPS)),
             dma,
+            dma((3,)),
             dma((3,)),
             dma,
             pltpu.SemaphoreType.REGULAR((3,)),

time: 69 us -> 68.6 us (level)
  the two profiles are of different devices: /device:TPU:1 before, /device:TPU:4 now
where the time goes in v8:
time: 68.6 us; the launch traced here: 68.5 us
  Pallas kernels  67.9 us (99%)
    pallas_call x1, Pallas kernels, shards(): pl.pallas_call(lambda *refs: kernel(scaling, *refs), out_shape=(pltpu.VME...  67.1 us

profile of v8, /device:TPU:4, one launch (start us, length us, event | category | flops | bytes accessed | tf_op | source)
XLA Modules:
  0.0 68.5 jit_solution(17356087321934199529)
XLA Ops:
  0.6 67.1 %residual_step.1 = (f32[3,128,80]{2,1,0:T(8,128)S(1)}, bf16[4,64,320]{2,1,0:T(8,128)(2,1)S(1)}) custom-call(bf16[4,64,320]{2,1,0:T(8,128)(2,1)} %bitcast.8, bf16[2,9,320,320]{3,2,1,0:T(8,128)(2,1)} %bitcast.7, bf16[4,64,320]{2,1,0:T(8,128)(2,1)} %bitcast.9), custom_call_target="tpu_custom_call" | custom-call | tf_op jit(solution)/shard_map/residual_step/pallas_call | solution.py:653
  67.7 0.8 %outputs.1 = (f32[9,20,2,80]{3,2,1,0:T(2,128)}, bf16[4,64,320]{2,1,0:T(8,128)(2,1)}) custom-call(f32[3,128,80]{2,1,0:T(8,128)S(1)} %get-tuple-element.6.gk, bf16[4,64,320]{2,1,0:T(8,128)(2,1)S(1)} %get-tuple-element.7.gi), custom_call_target="tpu_custom_call" | custom-call | tf_op jit(solution)/shard_map/outputs/pallas_call | solution.py:717

commit v9 on v8

--- a/solution.py
+++ b/solution.py
@@ -489,18 +489,27 @@
     at_end = s == SECTIONS - 1
 
     def step(i, carry):
-        turn = i - jnp.where(s == 0, CROPS, 2 * CROPS + ahead_count)
-
-        @pl.when((turn > 0) & (turn <= 3))
-        def _():
-            pl.semaphore_wait(token.at[turn - 1], 2)
-
-        @pl.when((turn >= 0) & (turn < 3))
-        def _():
+        def vouch(turn):
             for d in (1, CHIPS - 1):
                 pl.semaphore_signal(
                     token.at[turn], inc=1, device_id=chip_of(d), device_id_type=MESH
                 )
+
+        @pl.when((s >= 2) & (i == 0))
+        def _():
+            for turn in range(3):
+                vouch(turn)
+                pl.semaphore_wait(token.at[turn], 2)
+
+        turn = i - CROPS
+
+        @pl.when((s < 2) & (turn > 0) & (turn <= 3))
+        def _():
+            pl.semaphore_wait(token.at[turn - 1], 2)
+
+        @pl.when((s < 2) & (turn >= 0) & (turn < 3))
+        def _():
+            vouch(turn)
 
         back_from = CROPS + ahead_count
         is_forward = jnp.where(at_end, (i < 2 * CROPS) & (i % 2 == 0), i < CROPS)
@@ -545,8 +554,10 @@
         for half in range(2):
             for q in range(4):
                 pk[t, 4 * half + q] = packed[half, :, 128 * q : 128 * (q + 1)]
-        near, held = (1, 3) if t % 2 == 0 else (7, 5)
-        send_block((z + 4) % CHIPS, t, near, far.at[t], far_recv.at[t])
+        send_block((z + 4) % CHIPS, t, 1 if t % 2 == 0 else 7, far.at[t], far_recv.at[t])
+
+    def direct(t):
+        held = 3 if t % 2 == 0 else 5
         for slot, d in enumerate(DIRECT):
             if d != held:
                 send_block((z + d) % CHIPS, t, d, rz.at[t, slot], z_recv.at[t])
@@ -584,17 +595,20 @@
         @pl.when(i == 5)
         def _():
             pack(2)
+            direct(2)
 
         return carry
 
     lax.fori_loop(jnp.where(s == 0, 0, 5), 2 * CROPS, tail, 0)
     pack(1)
     pack(0)
+    direct(1)
+    direct(0)
     merge(2)
     merge(1)
     merge(0)
 
-    for t in (2, 1, 0):
+    for t in (2, 0, 1):
         waited(rz.at[t], z_recv.at[t])
         total = pk[t, z].astype(F32)
         for slot in range(len(DIRECT)):

time: 68.6 us -> 66.9 us (0.975)
  the two profiles are of different devices: /device:TPU:4 before, /device:TPU:1 now
where the time goes in v9:
time: 66.9 us
  Pallas kernels  66.2 us (99%)
    pallas_call x1, Pallas kernels, shards(): pl.pallas_call(lambda *refs: kernel(scaling, *refs), out_shape=(pltpu.VME...  65.4 us

profile of v9, /device:TPU:1, one launch (start us, length us, event | category | flops | bytes accessed | tf_op | source)
XLA Modules:
  0.0 66.9 jit_solution(14263075302253406090)
XLA Ops:
  0.6 65.4 %residual_step.1 = (f32[3,128,80]{2,1,0:T(8,128)S(1)}, bf16[4,64,320]{2,1,0:T(8,128)(2,1)S(1)}) custom-call(bf16[4,64,320]{2,1,0:T(8,128)(2,1)} %bitcast.8, bf16[2,9,320,320]{3,2,1,0:T(8,128)(2,1)} %bitcast.7, bf16[4,64,320]{2,1,0:T(8,128)(2,1)} %bitcast.9), custom_call_target="tpu_custom_call" | custom-call | tf_op jit(solution)/shard_map/residual_step/pallas_call | solution.py:667
  66.1 0.8 %outputs.1 = (f32[9,20,2,80]{3,2,1,0:T(2,128)}, bf16[4,64,320]{2,1,0:T(8,128)(2,1)}) custom-call(f32[3,128,80]{2,1,0:T(8,128)S(1)} %get-tuple-element.6.gk, bf16[4,64,320]{2,1,0:T(8,128)(2,1)S(1)} %get-tuple-element.7.gi), custom_call_target="tpu_custom_call" | custom-call | tf_op jit(solution)/shard_map/outputs/pallas_call | solution.py:731

commit v10 on v9

--- a/solution.py
+++ b/solution.py
@@ -423,7 +423,6 @@
                     device_id_type=MESH,
                 ).start()
 
-        gi_out[k] = permuted(swap, grad_in)
         lower = wide[8 : 8 + POS].astype(BF16)
         chunks = permuted(jnp.concatenate([lower, center.astype(BF16)], axis=0), sel[...])
         share_grad(0, k, chunks[:POS])
@@ -576,9 +575,6 @@
         def _():
             relay_grad(1, 2)
             relay_grad(0, 2)
-
-        @pl.when(first & (i == 4))
-        def _():
             relay_grad(1, last, IMAGES)
 
         @pl.when(first & (i == 6))
@@ -604,6 +600,8 @@
     pack(0)
     direct(1)
     direct(0)
+    for k in range(CROPS):
+        gi_out[k] = permuted(swap, gout[k])
     merge(2)
     merge(1)
     merge(0)

time: 66.9 us -> 66.6 us (level)
  no operation moved by 1% of the time
where the time goes in v10:
time: 66.6 us; the launch traced here: 66.5 us
  Pallas kernels  65.8 us (99%)
    pallas_call x1, Pallas kernels, shards(): pl.pallas_call(lambda *refs: kernel(scaling, *refs), out_shape=(pltpu.VME...  65.1 us

profile of v10, /device:TPU:1, one launch (start us, length us, event | category | flops | bytes accessed | tf_op | source)
XLA Modules:
  0.0 66.5 jit_solution(8621298238551622701)
XLA Ops:
  0.6 65.1 %residual_step.1 = (f32[3,128,80]{2,1,0:T(8,128)S(1)}, bf16[4,64,320]{2,1,0:T(8,128)(2,1)S(1)}) custom-call(bf16[4,64,320]{2,1,0:T(8,128)(2,1)} %bitcast.8, bf16[2,9,320,320]{3,2,1,0:T(8,128)(2,1)} %bitcast.7, bf16[4,64,320]{2,1,0:T(8,128)(2,1)} %bitcast.9), custom_call_target="tpu_custom_call" | custom-call | tf_op jit(solution)/shard_map/residual_step/pallas_call | solution.py:665
  65.7 0.8 %outputs.1 = (f32[9,20,2,80]{3,2,1,0:T(2,128)}, bf16[4,64,320]{2,1,0:T(8,128)(2,1)}) custom-call(f32[3,128,80]{2,1,0:T(8,128)S(1)} %get-tuple-element.6.gk, bf16[4,64,320]{2,1,0:T(8,128)(2,1)S(1)} %get-tuple-element.7.gi), custom_call_target="tpu_custom_call" | custom-call | tf_op jit(solution)/shard_map/outputs/pallas_call | solution.py:729
